TPU v7x, 128 devices: a whole 4x4x4 slice. The times are simulated.
128 devices in a mesh: tile: 32 (over z, x, core), slab: 4 (over y).
Axes of the slice: x: 4, y: 4, z: 4, core: 2. Of those that a mesh axis runs over, the one named last changes fastest.
Arguments:
- object_field: float32 [2, 2, 16384, 2048], P(None, None, 'tile', 'slab')
- probe: float32 [2, 256, 256], replicated, may hold values from -5 to 5
- kernel_phase: float32 [256, 256], replicated, may hold values from -3.140625 to 3.140625
- measured: float32 [512, 256, 256], P(('tile', 'slab')), may hold values from 0.2 to 2
- positions: int32 [512, 2], P(('tile', 'slab')), may hold values from 0 to 16128, as said below
- batch: int32 [512], P(('tile', 'slab')), may hold values from 0 to 1
Outputs:
- object_new: float32 [2, 2, 16384, 2048], P(None, None, 'tile', 'slab')
- probe_new: float32 [2, 256, 256], replicated
Inputs may be any that keep to these rules, and one draw needn't show every extreme that they name: `positions`: frame f's top-left pixel lies in the tile of rows t * 512 .. (t + 1) * 512 - 1 and columns s * 512 .. (s + 1) * 512 - 1, where t = (f // 4) // 4 and s = (f // 4) % 4; every frame lies inside the object.
All inputs are finite; a program needn't handle non-finite values.
Results may differ from a plain program's by a relative error of at most 0.0003.
Values sent between devices are 32-bit elements; how exact they have to be, the bound alone decides.
A program may use at most 192 MiB of HBM per device.

v0:
```python
import math

import jax
import jax.numpy as jnp
from jax import lax
from jax.sharding import PartitionSpec as P

BATCHES = 2


def shifted(value, axis, steps):
    count = lax.axis_size(axis)
    first, last = (max(0, -steps), min(count, count - steps))
    return lax.ppermute(value, axis, [(source, source + steps) for source in range(first, last)])


def packed_total(arrays, axis):
    vector, at, done = (jnp.concatenate([a.reshape(-1) for a in arrays]), 0, [])
    subtotal = lax.psum(vector, axis)
    for a in arrays:
        done.append(subtotal[at : at + a.size].reshape(a.shape))
        at += a.size
    return tuple(done)


def dft_tables(size):
    index = jnp.arange(size, dtype=jnp.int32)
    product = index[:, None] * index[None, :] % size
    angles = product.astype(jnp.float32) * (2.0 * math.pi / size)
    norm_scale = 1.0 / math.sqrt(size)
    return (jnp.cos(angles) * norm_scale, -jnp.sin(angles) * norm_scale)


def matmul_pair(left_real, left_imag, right_real, right_imag):
    first = jnp.matmul(left_real, right_real, precision=lax.Precision.HIGHEST) - jnp.matmul(
        left_imag, right_imag, precision=lax.Precision.HIGHEST
    )
    second = jnp.matmul(left_real, right_imag, precision=lax.Precision.HIGHEST) + jnp.matmul(
        left_imag, right_real, precision=lax.Precision.HIGHEST
    )
    return (first, second)


def fourier(real_part, imag_part, cos_table, sin_table):
    mid_real, mid_imag = matmul_pair(real_part, imag_part, cos_table, sin_table)
    return matmul_pair(cos_table, sin_table, mid_real, mid_imag)


def frame_pass(patches, probe, kernel, measured, tables):
    cos_table, sin_table = tables
    back_sin = -sin_table
    kernel_real, kernel_imag = kernel
    patch_real = patches[:, 0]
    patch_imag = patches[:, 1]
    layers = patches.shape[2]
    wave_real = probe[0] * patch_real[:, 0] - probe[1] * patch_imag[:, 0]
    wave_imag = probe[0] * patch_imag[:, 0] + probe[1] * patch_real[:, 0]
    layer = 1
    freq_real, freq_imag = fourier(wave_real, wave_imag, cos_table, sin_table)
    prop_real = freq_real * kernel_real - freq_imag * kernel_imag
    prop_imag = freq_real * kernel_imag + freq_imag * kernel_real
    in_real, in_imag = fourier(prop_real, prop_imag, cos_table, back_sin)
    incoming = [(in_real, in_imag)]
    wave_real = patch_real[:, layer] * in_real - patch_imag[:, layer] * in_imag
    wave_imag = patch_real[:, layer] * in_imag + patch_imag[:, layer] * in_real
    far_real, far_imag = fourier(wave_real, wave_imag, cos_table, sin_table)
    power = far_real * far_real + far_imag * far_imag
    factor = 1.0 - measured / jnp.sqrt(jnp.maximum(power, 0.01))
    grad_real, grad_imag = fourier(far_real * factor, far_imag * factor, cos_table, back_sin)
    layer_grads = [None] * layers
    layer = 1
    in_real, in_imag = incoming[layer - 1]
    layer_grads[layer] = (
        in_real * grad_real + in_imag * grad_imag,
        in_real * grad_imag - in_imag * grad_real,
    )
    back_real = patch_real[:, layer] * grad_real + patch_imag[:, layer] * grad_imag
    back_imag = patch_real[:, layer] * grad_imag - patch_imag[:, layer] * grad_real
    freq_real, freq_imag = fourier(back_real, back_imag, cos_table, sin_table)
    conj_real = freq_real * kernel_real + freq_imag * kernel_imag
    conj_imag = freq_imag * kernel_real - freq_real * kernel_imag
    grad_real, grad_imag = fourier(conj_real, conj_imag, cos_table, back_sin)
    layer_grads[0] = (
        probe[0] * grad_real + probe[1] * grad_imag,
        probe[0] * grad_imag - probe[1] * grad_real,
    )
    probe_grad = jnp.stack(
        [
            patch_real[:, 0] * grad_real + patch_imag[:, 0] * grad_imag,
            patch_real[:, 0] * grad_imag - patch_imag[:, 0] * grad_real,
        ],
        axis=1,
    )
    lighting = patch_real[:, 0] * patch_real[:, 0] + patch_imag[:, 0] * patch_imag[:, 0]
    object_grad = jnp.stack(
        [
            jnp.stack([item[0] for item in layer_grads], axis=1),
            jnp.stack([item[1] for item in layer_grads], axis=1),
        ],
        axis=1,
    )
    return (object_grad, probe_grad, lighting)


def take_columns(field, margin):
    edge = shifted(field[..., :margin], "slab", -1)
    return jnp.concatenate([field, edge], axis=3)


def take_rows(field, margin):
    edge = shifted(field[:, :, :margin, :], "tile", -1)
    return jnp.concatenate([field, edge], axis=2)


def give_rows(grads, margin):
    own_rows = grads.shape[2] - margin
    returned = shifted(grads[:, :, own_rows:, :], "tile", 1)
    kept = grads[:, :, :own_rows, :]
    return kept.at[:, :, :margin, :].add(returned)


def give_columns(grads, margin):
    own_cols = grads.shape[3] - margin
    returned = shifted(grads[..., own_cols:], "slab", 1)
    kept = grads[..., :own_cols]
    return kept.at[..., :margin].add(returned)


def shards(object_field, probe, kernel_phase, measured, positions, batch):
    side = probe.shape[-1]
    layers = object_field.shape[1]
    tile_rows = object_field.shape[2]
    tile_cols = object_field.shape[3]
    margin = side - 1
    tables = dft_tables(side)
    kernel = (jnp.cos(kernel_phase), jnp.sin(kernel_phase))
    corner = jnp.stack([lax.axis_index("tile") * tile_rows, lax.axis_index("slab") * tile_cols])
    local_at = positions - corner[None, :]
    zero = jnp.zeros((), jnp.int32)
    slots = positions.shape[0]
    current = object_field
    extended = object_field
    beam = probe
    for batch_no in range(BATCHES):
        extended = take_rows(take_columns(current, margin), margin)

        def cut_patch(where):
            return lax.dynamic_slice(
                extended, (zero, zero, where[0], where[1]), (2, layers, side, side)
            )

        patches = jax.vmap(cut_patch)(local_at)
        object_grad, probe_grad, lighting = frame_pass(patches, beam, kernel, measured, tables)
        weight = (batch == batch_no).astype(jnp.float32)
        object_grad = object_grad * weight[:, None, None, None, None]
        probe_sum = jnp.sum(probe_grad * weight[:, None, None, None], axis=0)
        light_sum = jnp.sum(lighting * weight[:, None, None], axis=0)

        def place(slot, grads):
            starts = (zero, zero, local_at[slot, 0], local_at[slot, 1])
            piece = lax.dynamic_slice(grads, starts, (2, layers, side, side)) + object_grad[slot]
            return lax.dynamic_update_slice(grads, piece, starts)

        wide_grads = lax.fori_loop(0, slots, place, jnp.zeros_like(extended))
        peak = jnp.max(beam[0] * beam[0] + beam[1] * beam[1])
        grads = give_columns(give_rows(wide_grads, margin), margin)
        current = current - grads / peak
        probe_total, light_total = packed_total((probe_sum, light_sum), ("tile", "slab"))
        beam = beam - probe_total / (light_total + 1.0)
    return (current, beam)


def solution(mesh):
    in_specs = (
        P(None, None, "tile", "slab"),
        P(),
        P(),
        P(("tile", "slab"), None, None),
        P(("tile", "slab"), None),
        P(("tile", "slab")),
    )
    out_specs = (P(None, None, "tile", "slab"), P())
    return jax.shard_map(shards, mesh=mesh, in_specs=in_specs, out_specs=out_specs, check_vma=False)
```

profile of v0, /device:TPU:1, one launch (start us, length us, event | category | flops | bytes accessed | tf_op | source)
XLA Modules:
  0.0 1102.0 jit_solution(2554224174085365021)
XLA Ops:
  12.5 7.4 copy.19
  19.9 40.4 %collective-permute-done = f32[2,2,512,255]{2,1,3,0:T(2,128)} collective-permute-done((f32[2,2,512,255]{2,1,3,0:T(2,128)}, f32[2,2,512,255]{2,1,3,0:T(2,128)}, u32[]{:S(2)}, u32[]{:S(2)}) %collective-permute-start) | collective-permute-done | bytes 2088992 | tf_op jit(solution)/shard_map/ppermute | solution.py:14
  60.3 4.7 copy.20
  65.1 4.7 pad_maximum_fusion.3
  75.3 34.3 %collective-permute-done.1 = f32[2,2,255,767]{3,1,2,0:T(2,128)} collective-permute-done((f32[2,2,255,767]{3,1,2,0:T(2,128)}, f32[2,2,255,767]{3,1,2,0:T(2,128)}, u32[]{:S(2)}, u32[]{:S(2)}) %collective-permute-start.1) | collective-permute-done | bytes 3129392 | tf_op jit(solution)/shard_map/ppermute | solution.py:14
  109.7 18.3 %pad_maximum_fusion.1 = f32[2,2,767,767]{3,1,2,0:T(2,128)} fusion(f32[2,2,255,767]{3,1,2,0:T(2,128)} %collective-permute-done.1, f32[2,2,512,255]{3,1,2,0:T(2,128)S(1)} %copy.20, f32[2,2,512,512]{3,1,2,0:T(2,128)} %copy.19), kind=kLoop, calls=%fused_computation.12 | loop fusion | flops 4706312 | bytes 18825248 | tf_op jit(solution)/shard_map/concatenate | solution.py:112
  130.4 22.6 %while.34 = (s32[]{:T(128)}, f32[2,2,767,767]{3,1,2,0:T(2,128)}, s32[4,4]{1,0:T(4,128)S(1)}, f32[4,2,2,256,256]{4,3,0,2,1:T(8,128)}, s32[]{:T(128)}) while((s32[]{:T(128)}, f32[2,2,767,767]{3,1,2,0:T(2,128)}, s32[4,4]{1,0:T(4,128)S(1)}, f32[4,2,2,256,256]{4,3,0,2,1:T(8,128)}, s32[]{:T(128)}) %tuple.140), condition=%wide.while_cond.4, body=%wide.while_body.4.sunk | while | flops 2 | bytes 4194937 | solution.py:148
  131.1 3.9 constant_dynamic-slice_fusion.15
  136.7 3.9 constant_dynamic-slice_fusion.15
  142.3 3.9 constant_dynamic-slice_fusion.15
  255.3 4.2 add_bitcast_fusion.3
  262.5 4.5 broadcast.145.clone
  267.0 75.2 %while.32 = (s32[]{:T(128)}, f32[2,2,767,767]{3,2,1,0:T(8,128)}, s32[4,2]{0,1:T(2,128)S(1)}, f32[4,2,2,256,256]{4,3,0,2,1:T(8,128)}, s32[]{:T(128)}, /*index=5*/s32[]{:T(128)}, s32[]{:T(128)}) while((s32[]{:T(128)}, f32[2,2,767,767]{3,2,1,0:T(8,128)}, s32[4,2]{0,1:T(2,128)S(1)}, f32[4,2,2,256,256]{4,3,0,2,1:T(8,128)}, s32[]{:T(128)}, ...), condition=%wide.region_1.2_spmd, body=%wide.region_0.1_spmd.sunk | while | flops 262152 | bytes 5243061 | solution.py:164
  273.7 11.9 %dynamic_update_slice.16 = f32[2,2,767,767]{3,2,1,0:T(8,128)} dynamic-update-slice(f32[2,2,767,767]{3,2,1,0:T(8,128)} %get-tuple-element.473, f32[2,2,256,256]{3,2,1,0:T(8,128)S(1)} %bitcast_add_fusion.4, s32[]{:T(128)} %constant.179.clone.1..sunk, s32[]{:T(128)} %constant.179.clone.1..sunk, s32[]{:T(128)S(6)} %select_n.573, s32[]{:T(128)S(6)} %select_n.574) | dynamic-update-slice | bytes 2097156 | tf_op jit(solution)/shard_map/while/body/eval_jaxpr/dynamic_update_slice | solution.py:162
  292.3 12.4 %dynamic_update_slice.16 = f32[2,2,767,767]{3,2,1,0:T(8,128)} dynamic-update-slice(f32[2,2,767,767]{3,2,1,0:T(8,128)} %get-tuple-element.473, f32[2,2,256,256]{3,2,1,0:T(8,128)S(1)} %bitcast_add_fusion.4, s32[]{:T(128)} %constant.179.clone.1..sunk, s32[]{:T(128)} %constant.179.clone.1..sunk, s32[]{:T(128)S(6)} %select_n.573, s32[]{:T(128)S(6)} %select_n.574) | dynamic-update-slice | bytes 2097156 | tf_op jit(solution)/shard_map/while/body/eval_jaxpr/dynamic_update_slice | solution.py:162
  311.4 12.0 %dynamic_update_slice.16 = f32[2,2,767,767]{3,2,1,0:T(8,128)} dynamic-update-slice(f32[2,2,767,767]{3,2,1,0:T(8,128)} %get-tuple-element.473, f32[2,2,256,256]{3,2,1,0:T(8,128)S(1)} %bitcast_add_fusion.4, s32[]{:T(128)} %constant.179.clone.1..sunk, s32[]{:T(128)} %constant.179.clone.1..sunk, s32[]{:T(128)S(6)} %select_n.573, s32[]{:T(128)S(6)} %select_n.574) | dynamic-update-slice | bytes 2097156 | tf_op jit(solution)/shard_map/while/body/eval_jaxpr/dynamic_update_slice | solution.py:162
  330.1 12.0 %dynamic_update_slice.16 = f32[2,2,767,767]{3,2,1,0:T(8,128)} dynamic-update-slice(f32[2,2,767,767]{3,2,1,0:T(8,128)} %get-tuple-element.473, f32[2,2,256,256]{3,2,1,0:T(8,128)S(1)} %bitcast_add_fusion.4, s32[]{:T(128)} %constant.179.clone.1..sunk, s32[]{:T(128)} %constant.179.clone.1..sunk, s32[]{:T(128)S(6)} %select_n.573, s32[]{:T(128)S(6)} %select_n.574) | dynamic-update-slice | bytes 2097156 | tf_op jit(solution)/shard_map/while/body/eval_jaxpr/dynamic_update_slice | solution.py:162
  346.9 6.0 slice.324
  352.9 28.1 %collective-permute-done.2 = f32[2,2,255,767]{3,2,1,0:T(8,128)S(1)} collective-permute-done((f32[2,2,255,767]{3,2,1,0:T(8,128)S(1)}, f32[2,2,255,767]{3,2,1,0:T(8,128)S(1)}, u32[]{:S(2)}, u32[]{:S(2)}) %collective-permute-start.2) | collective-permute-done | bytes 3129392 | tf_op jit(solution)/shard_map/ppermute | solution.py:14
  381.1 4.2 slice_add_fusion.1
  385.3 8.8 scatter-add.14
  400.1 4.6 slice.394
  404.7 17.5 %collective-permute-done.3 = f32[2,2,512,255]{3,2,1,0:T(8,128)S(1)} collective-permute-done((f32[2,2,512,255]{3,2,1,0:T(8,128)S(1)}, f32[2,2,512,255]{3,2,1,0:T(8,128)S(1)}, u32[]{:S(2)}, u32[]{:S(2)}) %collective-permute-start.3) | collective-permute-done | bytes 2088992 | tf_op jit(solution)/shard_map/ppermute | solution.py:14
  425.4 11.1 %scatter-add.15 = f32[2,2,512,512]{3,2,1,0:T(8,128)} dynamic-update-slice(f32[2,2,512,512]{3,2,1,0:T(8,128)} %slice.394, f32[2,2,512,255]{3,2,1,0:T(8,128)} %slice_add_fusion.3, s32[]{:T(128)} %constant.179.clone.1, s32[]{:T(128)} %constant.179.clone.1, s32[]{:T(128)} %constant.179.clone.1, s32[]{:T(128)} %constant.179.clone.1) | dynamic-update-slice | bytes 4177924 | tf_op jit(solution)/shard_map/scatter-add | solution.py:126
  436.5 5.1 divide_subtract_fusion.1
  445.3 24.5 %collective-permute-done.4 = f32[2,2,512,255]{3,2,1,0:T(8,128)S(1)} collective-permute-done((f32[2,2,512,255]{3,2,1,0:T(8,128)S(1)}, f32[2,2,512,255]{3,2,1,0:T(8,128)S(1)}, u32[]{:S(2)}, u32[]{:S(2)}) %collective-permute-start.4) | collective-permute-done | bytes 2088992 | tf_op jit(solution)/shard_map/ppermute | solution.py:14
  475.1 202.9 %all-reduce.3.cloned.1.call-done = f32[196608]{0:T(1024)} async-done(((f32[196608]{0:T(1024)}), f32[196608]{0:T(1024)}) %all-reduce.3.cloned.1.call-update) | async-done | bytes 786448 | tf_op jit(solution)/shard_map/psum | solution.py:19
  681.2 8.4 pad_maximum_fusion
  692.1 19.4 %while.35 = (s32[]{:T(128)}, f32[2,2,767,767]{3,2,1,0:T(8,128)}, s32[4,4]{1,0:T(4,128)S(1)}, f32[4,2,2,256,256]{4,3,0,2,1:T(8,128)}, s32[]{:T(128)}) while((s32[]{:T(128)}, f32[2,2,767,767]{3,2,1,0:T(8,128)}, s32[4,4]{1,0:T(4,128)S(1)}, f32[4,2,2,256,256]{4,3,0,2,1:T(8,128)}, s32[]{:T(128)}) %tuple.157), condition=%wide.while_cond.5, body=%wide.while_body.5.sunk | while | flops 2 | bytes 2098801 | solution.py:148
  692.8 4.1 bitcast_dynamic-update-slice_fusion.5
  697.6 4.1 bitcast_dynamic-update-slice_fusion.5
  702.3 4.1 bitcast_dynamic-update-slice_fusion.5
  707.1 4.1 bitcast_dynamic-update-slice_fusion.5
  820.4 4.5 broadcast.145
  824.9 75.1 %while.33 = (s32[]{:T(128)}, f32[2,2,767,767]{3,2,1,0:T(8,128)}, s32[4,2]{0,1:T(2,128)S(1)}, f32[4,2,2,256,256]{4,3,0,2,1:T(8,128)}, s32[]{:T(128)}, /*index=5*/s32[]{:T(128)}, s32[]{:T(128)}) while((s32[]{:T(128)}, f32[2,2,767,767]{3,2,1,0:T(8,128)}, s32[4,2]{0,1:T(2,128)S(1)}, f32[4,2,2,256,256]{4,3,0,2,1:T(8,128)}, s32[]{:T(128)}, ...), condition=%wide.region_7.8_spmd, body=%wide.region_6.7_spmd.sunk | while | flops 262152 | bytes 5243061 | solution.py:164
  831.6 11.9 %dynamic_update_slice.17 = f32[2,2,767,767]{3,2,1,0:T(8,128)} dynamic-update-slice(f32[2,2,767,767]{3,2,1,0:T(8,128)} %get-tuple-element.509, f32[2,2,256,256]{3,2,1,0:T(8,128)S(1)} %bitcast_add_fusion.5, s32[]{:T(128)} %constant.179.clone.1..sunk.1, s32[]{:T(128)} %constant.179.clone.1..sunk.1, s32[]{:T(128)S(6)} %select_n.575, s32[]{:T(128)S(6)} %select_n.576) | dynamic-update-slice | bytes 2097156 | tf_op jit(solution)/shard_map/while/body/eval_jaxpr/dynamic_update_slice | solution.py:162
  850.2 12.4 %dynamic_update_slice.17 = f32[2,2,767,767]{3,2,1,0:T(8,128)} dynamic-update-slice(f32[2,2,767,767]{3,2,1,0:T(8,128)} %get-tuple-element.509, f32[2,2,256,256]{3,2,1,0:T(8,128)S(1)} %bitcast_add_fusion.5, s32[]{:T(128)} %constant.179.clone.1..sunk.1, s32[]{:T(128)} %constant.179.clone.1..sunk.1, s32[]{:T(128)S(6)} %select_n.575, s32[]{:T(128)S(6)} %select_n.576) | dynamic-update-slice | bytes 2097156 | tf_op jit(solution)/shard_map/while/body/eval_jaxpr/dynamic_update_slice | solution.py:162
  869.3 12.0 %dynamic_update_slice.17 = f32[2,2,767,767]{3,2,1,0:T(8,128)} dynamic-update-slice(f32[2,2,767,767]{3,2,1,0:T(8,128)} %get-tuple-element.509, f32[2,2,256,256]{3,2,1,0:T(8,128)S(1)} %bitcast_add_fusion.5, s32[]{:T(128)} %constant.179.clone.1..sunk.1, s32[]{:T(128)} %constant.179.clone.1..sunk.1, s32[]{:T(128)S(6)} %select_n.575, s32[]{:T(128)S(6)} %select_n.576) | dynamic-update-slice | bytes 2097156 | tf_op jit(solution)/shard_map/while/body/eval_jaxpr/dynamic_update_slice | solution.py:162
  888.0 12.0 %dynamic_update_slice.17 = f32[2,2,767,767]{3,2,1,0:T(8,128)} dynamic-update-slice(f32[2,2,767,767]{3,2,1,0:T(8,128)} %get-tuple-element.509, f32[2,2,256,256]{3,2,1,0:T(8,128)S(1)} %bitcast_add_fusion.5, s32[]{:T(128)} %constant.179.clone.1..sunk.1, s32[]{:T(128)} %constant.179.clone.1..sunk.1, s32[]{:T(128)S(6)} %select_n.575, s32[]{:T(128)S(6)} %select_n.576) | dynamic-update-slice | bytes 2097156 | tf_op jit(solution)/shard_map/while/body/eval_jaxpr/dynamic_update_slice | solution.py:162
  900.0 3.9 slice.345
  903.9 4.3 collective-permute-start.6
  908.2 6.0 slice.343
  916.0 27.8 %collective-permute-done.6 = f32[2,2,255,767]{3,2,1,0:T(8,128)} collective-permute-done((f32[2,2,255,767]{3,2,1,0:T(8,128)}, f32[2,2,255,767]{3,2,1,0:T(8,128)}, u32[]{:S(2)}, u32[]{:S(2)}) %collective-permute-start.6) | collective-permute-done | bytes 3129392 | tf_op jit(solution)/shard_map/ppermute | solution.py:14
  947.1 8.2 scatter-add.16
  961.3 102.2 %all-reduce.5.cloned.1.call-done = f32[196608]{0:T(1024)} async-done(((f32[196608]{0:T(1024)}), f32[196608]{0:T(1024)}) %all-reduce.5.cloned.1.call-update) | async-done | bytes 786448 | tf_op jit(solution)/shard_map/psum | solution.py:19
  1070.2 4.6 slice.406
  1077.2 10.5 scatter-add.19
  1087.8 7.2 divide_subtract_fusion
  (225 shorter events, 311.0 us)
Async XLA Ops:
  7.2 1.6 slice-start
  7.2 670.8 %all-reduce.3.cloned.1.call-start = ((), (), s32[]{:S(2)}) async-start(), calls=%async_computation | async-start | bytes 1572864 | tf_op jit(solution)/shard_map/psum | solution.py:19
  11.2 49.1 %collective-permute-start = (f32[2,2,512,255]{2,1,3,0:T(2,128)}, f32[2,2,512,255]{2,1,3,0:T(2,128)}, u32[]{:S(2)}, u32[]{:S(2)}) collective-permute-start(f32[2,2,512,255]{2,1,3,0:T(2,128)} %copy.37), channel_id=1, source_target_pairs={{1,0},{2,1},{3,2},{5,4},{6,5},{7,6},{9,8},{10,9},{11,10},{13,12},{... | collective-permute-start | bytes 6266888 | tf_op jit(solution)/shard_map/ppermute | solution.py:14
  65.0 8.2 copy-start.12
  65.1 8.5 copy-start.13
  65.1 9.2 copy-start.5
  65.1 9.3 copy-start.10
  69.8 39.9 %collective-permute-start.1 = (f32[2,2,255,767]{3,1,2,0:T(2,128)}, f32[2,2,255,767]{3,1,2,0:T(2,128)}, u32[]{:S(2)}, u32[]{:S(2)}) collective-permute-start(f32[2,2,255,767]{3,1,2,0:T(2,128)} %pad_maximum_fusion.3), channel_id=1, source_target_pairs={{4,0},{8,4},{12,8},{16,12},{20,16},{24,20},{28,24},{32,28},{36,32}... | collective-permute-start | bytes 9388088 | tf_op jit(solution)/shard_map/ppermute | solution.py:14
  201.6 4.4 copy-start.1
  344.3 36.8 %collective-permute-start.2 = (f32[2,2,255,767]{3,2,1,0:T(8,128)S(1)}, f32[2,2,255,767]{3,2,1,0:T(8,128)S(1)}, u32[]{:S(2)}, u32[]{:S(2)}) collective-permute-start(f32[2,2,255,767]{3,2,1,0:T(8,128)S(1)} %slice.326), channel_id=1, source_target_pairs={{0,4},{4,8},{8,12},{12,16},{16,20},{20,24},{24,28},{28,32},{32,36}... | collective-permute-start | bytes 9388088 | tf_op jit(solution)/shard_map/ppermute | solution.py:14
  394.1 5.4 copy-start.6
  395.8 26.4 %collective-permute-start.3 = (f32[2,2,512,255]{3,2,1,0:T(8,128)S(1)}, f32[2,2,512,255]{3,2,1,0:T(8,128)S(1)}, u32[]{:S(2)}, u32[]{:S(2)}) collective-permute-start(f32[2,2,512,255]{3,2,1,0:T(8,128)S(1)} %slice.396), channel_id=1, source_target_pairs={{0,1},{1,2},{2,3},{4,5},{5,6},{6,7},{8,9},{9,10},{10,11},{12,13},{... | collective-permute-start | bytes 6266888 | tf_op jit(solution)/shard_map/ppermute | solution.py:14
  441.6 28.2 %copy-start = (f32[2,2,512,512]{3,2,1,0:T(8,128)}, f32[2,2,512,512]{3,2,1,0:T(8,128)S(1)}, u32[]{:S(2)}) copy-start(f32[2,2,512,512]{3,2,1,0:T(8,128)S(1)} %divide_subtract_fusion.1) | copy-start | bytes 12582916
  441.6 2.0 copy-start.7
  441.7 3.0 copy-start.8
  441.9 27.9 %collective-permute-start.4 = (f32[2,2,512,255]{3,2,1,0:T(8,128)S(1)}, f32[2,2,512,255]{3,2,1,0:T(8,128)S(1)}, u32[]{:S(2)}, u32[]{:S(2)}) collective-permute-start(f32[2,2,512,255]{3,2,1,0:T(8,128)S(1)} %slice.400), channel_id=1, source_target_pairs={{1,0},{2,1},{3,2},{5,4},{6,5},{7,6},{9,8},{10,9},{11,10},{13,12},{... | collective-permute-start | bytes 6266888 | tf_op jit(solution)/shard_map/ppermute | solution.py:14
  469.8 2.3 copy-start.4
  472.1 209.0 %collective-permute-start.5 = (f32[2,2,255,767]{3,2,1,0:T(8,128)}, f32[2,2,255,767]{3,2,1,0:T(8,128)}, u32[]{:S(2)}, u32[]{:S(2)}) collective-permute-start(f32[2,2,255,767]{3,2,1,0:T(8,128)} %pad_maximum_fusion.2), channel_id=1, source_target_pairs={{4,0},{8,4},{12,8},{16,12},{20,16},{24,20},{28,24},{32,28},{36,32}... | collective-permute-start | bytes 9388088 | tf_op jit(solution)/shard_map/ppermute | solution.py:14
  475.0 588.5 %all-reduce.5.cloned.1.call-start = ((), (), s32[]{:S(2)}) async-start(), calls=%async_computation.1 | async-start | bytes 1572864 | tf_op jit(solution)/shard_map/psum | solution.py:19
  680.3 0.8 copy-start.2
  809.3 4.3 copy-start.11
  903.9 10.3 copy-start.9
  903.9 39.9 %collective-permute-start.6 = (f32[2,2,255,767]{3,2,1,0:T(8,128)}, f32[2,2,255,767]{3,2,1,0:T(8,128)}, u32[]{:S(2)}, u32[]{:S(2)}) collective-permute-start(f32[2,2,255,767]{3,2,1,0:T(8,128)} %slice.345), channel_id=1, source_target_pairs={{0,4},{4,8},{8,12},{12,16},{16,20},{20,24},{24,28},{28,32},{32,36}... | collective-permute-start | bytes 9388088 | tf_op jit(solution)/shard_map/ppermute | solution.py:14
  955.3 5.3 copy-start.3
  957.1 117.7 %collective-permute-start.7 = (f32[2,2,512,255]{3,2,1,0:T(8,128)S(1)}, f32[2,2,512,255]{3,2,1,0:T(8,128)}, u32[]{:S(2)}, u32[]{:S(2)}) collective-permute-start(f32[2,2,512,255]{3,2,1,0:T(8,128)S(1)} %slice.408), channel_id=1, source_target_pairs={{0,1},{1,2},{2,3},{4,5},{5,6},{6,7},{8,9},{9,10},{10,11},{12,13},{... | collective-permute-start | bytes 6266888 | tf_op jit(solution)/shard_map/ppermute | solution.py:14
Sparse Core Ops, SparseCore 0:
  475.2 202.7 all-reduce.2
  916.1 147.3 all-reduce.4
where the time goes:
time: 1110 us; the launch traced here: 1100 us
  waiting for transfers between devices  478 us (43%)
  local copies, waits for them, and re-layouts  258 us (23%)
  matrix products  206 us (19%)
  other arithmetic  90.2 us (8%)
  loops' own time  32.1 us (3%)
  starting transfers between devices  22.2 us (2%)
  between operations  15.4 us (1%)
    psum x2, waiting for transfers between devices, packed_total(): subtotal = lax.psum(vector, axis)  305 us
    ppermute x8, waiting for transfers between devices, shifted(): lax.ppermute(value, axis, [(source, source + steps) for source in range(f...  173 us
    dynamic_update_slice x8, local copies, waits for them, and re-layouts, place(): return lax.dynamic_update_slice(grads, piece, starts)  96.5 us
    dot_general x24, matrix products, matmul_pair(): jnp.matmul(left_imag, right_imag, precision=lax.Precision.HIGHEST)  55.9 us
    dot_general x24, matrix products, matmul_pair(): jnp.matmul(left_imag, right_real, precision=lax.Precision.HIGHEST)  50.4 us
    dot_general x24, matrix products, matmul_pair(): jnp.matmul(left_real, right_real, precision=lax.Precision.HIGHEST)  50.1 us
    dot_general x24, matrix products, matmul_pair(): jnp.matmul(left_real, right_imag, precision=lax.Precision.HIGHEST)  49.7 us
    gather x28, local copies, waits for them, and re-layouts  41.5 us
  transfers between devices with their start and end apart: 10, of which 8 were waited for; matrix products, arithmetic and copies ran while one was open for 5% of the time, Pallas kernels for 0%

commit v1 on v0

v1 whole, which is shorter than its diff:
```python
import functools
import math

import jax
import jax.numpy as jnp
import numpy as np
from jax import lax
from jax.experimental import pallas as pl
from jax.experimental.pallas import tpu as pltpu
from jax.sharding import PartitionSpec as P

BATCHES = 2
K = 256
HALF = 128
F32 = jnp.float32
BF16 = jnp.bfloat16


def shifted(value, axis, steps):
    count = lax.axis_size(axis)
    first, last = (max(0, -steps), min(count, count - steps))
    return lax.ppermute(value, axis, [(source, source + steps) for source in range(first, last)])


def packed_total(value, axis):
    return lax.psum(value.reshape(-1), axis).reshape(value.shape)


def bf16_pair(table):
    table = jnp.asarray(table, F32)
    high = table.astype(BF16)
    low = (table - high.astype(F32)).astype(BF16)
    return high, low


def constants():
    index = np.arange(HALF)
    angle = 2.0 * np.pi * (np.outer(index, index) % HALF) / HALF
    cos, sin = np.cos(angle) / 16.0, -np.sin(angle) / 16.0
    right = np.block([[cos, sin], [-sin, cos]])
    right_inv = np.block([[cos, -sin], [sin, cos]])
    rights, lefts = [], []
    for table in (right, right_inv):
        high, low = bf16_pair(table)
        rights.append(jnp.concatenate([high, low, high], axis=0))
        high, low = bf16_pair(table.T)
        lefts.append(jnp.concatenate([high, low, high], axis=1))
    twist = 2.0 * np.pi * index / K
    wr, wi = np.cos(twist).astype(np.float32), -np.sin(twist).astype(np.float32)
    lanes = jnp.asarray(np.stack([np.broadcast_to(wr, (8, HALF)), np.broadcast_to(wi, (8, HALF))]))
    rows = jnp.asarray(np.stack([np.broadcast_to(wr[:, None], (HALF, HALF)), np.broadcast_to(wi[:, None], (HALF, HALF))]))
    return (jnp.stack(rights), jnp.stack(lefts), lanes, rows)


def even_odd(value):
    order = np.concatenate([np.arange(0, K, 2), np.arange(1, K, 2)])
    pick = np.zeros((K, K), np.float32)
    pick[order, np.arange(K)] = 1.0
    pick = jnp.asarray(pick)
    value = jnp.matmul(value, pick, precision=lax.Precision.HIGHEST)
    return jnp.einsum("kn,...kc->...nc", pick, value, precision=lax.Precision.HIGHEST)


def batch_kernel(
    batch_no, at_ref, which_ref, own_ref, right_ref, below_ref, corner_ref, beam_ref, kern_ref, meas_ref,
    mr_ref, ml_ref, wl_ref, wr_ref,
    g_own, g_right, g_below, g_corner, es_ref,
    ext, grad, patch, quantity, urh, url, ulh, ull, vr, vl, sems,
):
    tile = 2 * K
    parts = [
        (own_ref, g_own, pl.ds(0, tile), pl.ds(0, tile)),
        (right_ref, g_right, pl.ds(0, tile), pl.ds(tile, K)),
        (below_ref, g_below, pl.ds(tile, K), pl.ds(0, tile)),
        (corner_ref, g_corner, pl.ds(tile, K), pl.ds(tile, K)),
    ]
    copies = [
        pltpu.make_async_copy(src, ext.at[:, :, rows, cols], sems.at[n]) for n, (src, _, rows, cols) in enumerate(parts)
    ]
    for copy in copies:
        copy.start()
    def clear(i, carry):
        rows = pl.ds(pl.multiple_of(i * 64, 64), 64)
        for c in range(2):
            for layer in range(2):
                grad[c, layer, rows, :] = jnp.zeros((64, 3 * K), F32)
        return carry

    lax.fori_loop(0, 12, clear, 0)
    es_ref[...] = jnp.zeros_like(es_ref)
    for copy in copies:
        copy.wait()

    lane = lax.broadcasted_iota(jnp.int32, (8, HALF), 1)
    sub = lax.broadcasted_iota(jnp.int32, (8, HALF), 0)
    lo, hi = slice(0, HALF), slice(HALF, K)

    def split_to(high_ref, low_ref, rows, cols, value):
        high = value.astype(BF16)
        high_ref[rows, cols] = high
        low_ref[rows, cols] = (value - high.astype(F32)).astype(BF16)

    def dot_right(inverse):
        left = jnp.concatenate([urh[...], urh[...], url[...]], axis=1)
        vr[...] = jnp.dot(left, mr_ref[inverse], preferred_element_type=F32)

    def dot_left(inverse):
        right = jnp.concatenate([ulh[...], ulh[...], ull[...]], axis=0)
        vl[...] = jnp.dot(ml_ref[inverse], right, preferred_element_type=F32)

    def right_in(i, n, ar, ai, br, bi):
        wr, wi = wl_ref[0, 0:1, :], wl_ref[1, 0:1, :]
        dr, di = ar - br, ai - bi
        split_to(urh, url, slice(i, i + n), lo, ar + br)
        split_to(urh, url, slice(i, i + n), hi, ai + bi)
        split_to(urh, url, slice(K + i, K + i + n), lo, dr * wr - di * wi)
        split_to(urh, url, slice(K + i, K + i + n), hi, dr * wi + di * wr)

    def right_out(i, n):
        wr, wi = wl_ref[0, 0:1, :], wl_ref[1, 0:1, :]
        er, ei = vr[i : i + n, lo], vr[i : i + n, hi]
        our, oi = vr[K + i : K + i + n, lo], vr[K + i : K + i + n, hi]
        tr, ti = our * wr + oi * wi, oi * wr - our * wi
        return er + tr, ei + ti, er - tr, ei - ti

    def left_in():
        for i in range(0, HALF, 32):
            wr, wi = wr_ref[0, i : i + 32, :], wr_ref[1, i : i + 32, :]
            for cb in range(2):
                top, low = slice(cb * K + i, cb * K + i + 32), slice(cb * K + HALF + i, cb * K + HALF + i + 32)
                ar, ai, br, bi = vr[top, lo], vr[top, hi], vr[low, lo], vr[low, hi]
                dr, di = ar - br, ai - bi
                even, odd = slice(cb * HALF, cb * HALF + HALF), slice(K + cb * HALF, K + cb * HALF + HALF)
                split_to(ulh, ull, slice(i, i + 32), even, ar + br)
                split_to(ulh, ull, slice(HALF + i, HALF + i + 32), even, ai + bi)
                split_to(ulh, ull, slice(i, i + 32), odd, dr * wr - di * wi)
                split_to(ulh, ull, slice(HALF + i, HALF + i + 32), odd, dr * wi + di * wr)

    def left_out():
        for i in range(0, HALF, 32):
            wr, wi = wr_ref[0, i : i + 32, :], wr_ref[1, i : i + 32, :]
            for cb in range(2):
                even, odd = slice(cb * HALF, cb * HALF + HALF), slice(K + cb * HALF, K + cb * HALF + HALF)
                rr, ii = slice(i, i + 32), slice(HALF + i, HALF + i + 32)
                er, ei, our, oi = vl[rr, even], vl[ii, even], vl[rr, odd], vl[ii, odd]
                tr, ti = our * wr + oi * wi, oi * wr - our * wi
                top, low = slice(cb * K + i, cb * K + i + 32), slice(cb * K + HALF + i, cb * K + HALF + i + 32)
                split_to(urh, url, top, lo, er + tr)
                split_to(urh, url, top, hi, ei + ti)
                split_to(urh, url, low, lo, er - tr)
                split_to(urh, url, low, hi, ei - ti)

    def at_frequency(change):
        for i in range(0, HALF, 32):
            for kb in range(2):
                for cb in range(2):
                    cols = slice(kb * K + cb * HALF, kb * K + cb * HALF + HALF)
                    rr, ii = slice(i, i + 32), slice(HALF + i, HALF + i + 32)
                    at = (slice(kb * HALF + i, kb * HALF + i + 32), slice(cb * HALF, cb * HALF + HALF))
                    re, im = change(vl[rr, cols], vl[ii, cols], at)
                    split_to(ulh, ull, rr, cols, re)
                    split_to(ulh, ull, ii, cols, im)

    def propagate(re, im, at):
        kr, ki = kern_ref[0][at], kern_ref[1][at]
        return re * kr - im * ki, re * ki + im * kr

    def propagate_back(re, im, at):
        kr, ki = kern_ref[0][at], kern_ref[1][at]
        return re * kr + im * ki, im * kr - re * ki

    def frame(f, carry):
        @pl.when(which_ref[f] == batch_no)
        def _():
            row, col = at_ref[f, 0], at_ref[f, 1]
            row_base = pl.multiple_of((row // 8) * 8, 8)
            col_base = pl.multiple_of((col // HALF) * HALF, HALF)
            down, off = row - row_base, col - col_base
            up, back = lax.rem(8 - down, 8), lax.rem(HALF - off, HALF)
            keep, keep_row = lane < HALF - off, sub < 8 - down
            inside, inside_row = lane >= off, sub >= down
            zero = jnp.zeros((8, HALF), F32)

            def window(i, j):
                return pl.ds(pl.multiple_of(row_base + i, 8), 8), pl.ds(pl.multiple_of(col_base + j * HALF, HALF), HALF)

            def cut(step, carry):
                i = step * 32
                for c in range(2):
                    for layer in range(2):
                        columns = []
                        for j in range(3):
                            turned = [
                                pltpu.roll(pltpu.roll(ext[(c, layer) + window(i + 8 * k, j)], back, 1), up, 0) for k in range(5)
                            ]
                            columns.append([jnp.where(keep_row, turned[k], turned[k + 1]) for k in range(4)])
                        for k in range(4):
                            at = pl.ds(pl.multiple_of(i + 8 * k, 8), 8)
                            patch[c, layer, at, lo] = jnp.where(keep, columns[0][k], columns[1][k])
                            patch[c, layer, at, hi] = jnp.where(keep, columns[1][k], columns[2][k])
                return carry

            lax.fori_loop(0, K // 32, cut, 0)

            def place(layer, i, half_r, half_i):
                for c, halves in enumerate((half_r, half_i)):
                    turned = [
                        [pltpu.roll(pltpu.roll(half[8 * k : 8 * k + 8], off, 1), down, 0) for k in range(4)] for half in halves
                    ]
                    left, right = [
                        [
                            jnp.where(inside_row, side[k] if k < 4 else zero, side[k - 1] if k else zero)
                            for k in range(5)
                        ]
                        for side in turned
                    ]
                    for k in range(5):
                        adds = (
                            jnp.where(inside, left[k], zero),
                            jnp.where(inside, right[k], left[k]),
                            jnp.where(inside, zero, right[k]),
                        )
                        for j, add in enumerate(adds):
                            at = (c, layer) + window(i + 8 * k, j)
                            grad[at] = grad[at] + add

            for i in range(0, K, 32):
                rows = slice(i, i + 32)
                waves = []
                for cols in (lo, hi):
                    br, bi = beam_ref[0, rows, cols], beam_ref[1, rows, cols]
                    pr, pi = patch[0, 0, rows, cols], patch[1, 0, rows, cols]
                    waves += [br * pr - bi * pi, br * pi + bi * pr]
                    es_ref[2, rows, cols] = es_ref[2, rows, cols] + (pr * pr + pi * pi)
                right_in(i, 32, *waves)
            dot_right(0)
            left_in()
            dot_left(0)
            at_frequency(propagate)
            dot_left(1)
            left_out()
            dot_right(1)
            for i in range(0, K, 32):
                rows = slice(i, i + 32)
                qs = right_out(i, 32)
                waves = []
                for n, cols in enumerate((lo, hi)):
                    qr, qi = qs[2 * n], qs[2 * n + 1]
                    quantity[0, rows, cols] = qr
                    quantity[1, rows, cols] = qi
                    pr, pi = patch[0, 1, rows, cols], patch[1, 1, rows, cols]
                    waves += [pr * qr - pi * qi, pr * qi + pi * qr]
                right_in(i, 32, *waves)
            dot_right(0)
            left_in()
            dot_left(0)

            def residual(re, im, at):
                power = re * re + im * im
                factor = 1.0 - meas_ref[f, at[0], at[1]] * lax.rsqrt(jnp.maximum(power, 0.01))
                return re * factor, im * factor

            at_frequency(residual)
            dot_left(1)
            left_out()
            dot_right(1)
            for i in range(0, K, 32):
                rows = slice(i, i + 32)
                gs = right_out(i, 32)
                waves, dr, di = [], [], []
                for n, cols in enumerate((lo, hi)):
                    gr, gi = gs[2 * n], gs[2 * n + 1]
                    qr, qi = quantity[0, rows, cols], quantity[1, rows, cols]
                    pr, pi = patch[0, 1, rows, cols], patch[1, 1, rows, cols]
                    dr.append(qr * gr + qi * gi)
                    di.append(qr * gi - qi * gr)
                    waves += [pr * gr + pi * gi, pr * gi - pi * gr]
                right_in(i, 32, *waves)
                place(1, i, dr, di)
            dot_right(0)
            left_in()
            dot_left(0)
            at_frequency(propagate_back)
            dot_left(1)
            left_out()
            dot_right(1)
            for i in range(0, K, 32):
                rows = slice(i, i + 32)
                gs = right_out(i, 32)
                dr, di = [], []
                for n, cols in enumerate((lo, hi)):
                    gr, gi = gs[2 * n], gs[2 * n + 1]
                    br, bi = beam_ref[0, rows, cols], beam_ref[1, rows, cols]
                    pr, pi = patch[0, 0, rows, cols], patch[1, 0, rows, cols]
                    dr.append(br * gr + bi * gi)
                    di.append(br * gi - bi * gr)
                    es_ref[0, rows, cols] = es_ref[0, rows, cols] + (pr * gr + pi * gi)
                    es_ref[1, rows, cols] = es_ref[1, rows, cols] + (pr * gi - pi * gr)
                place(0, i, dr, di)

        return carry

    lax.fori_loop(0, which_ref.shape[0], frame, 0)
    backs = [
        pltpu.make_async_copy(grad.at[:, :, rows, cols], dst, sems.at[n]) for n, (_, dst, rows, cols) in enumerate(parts)
    ]
    for copy in backs:
        copy.start()
    for copy in backs:
        copy.wait()


def run_batch(batch_no, local_at, batch, pieces, beam, kern, meas, tables):
    tile = 2 * K
    smem = pl.BlockSpec(memory_space=pltpu.SMEM)
    vmem = pl.BlockSpec(memory_space=pltpu.VMEM)
    anyw = pl.BlockSpec(memory_space=pl.ANY)
    shapes = [(2, 2, tile, tile), (2, 2, tile, K), (2, 2, K, tile), (2, 2, K, K)]
    return pl.pallas_call(
        functools.partial(batch_kernel, batch_no),
        out_shape=[jax.ShapeDtypeStruct(s, F32) for s in shapes] + [jax.ShapeDtypeStruct((3, K, K), F32)],
        in_specs=[smem, smem] + [anyw] * 4 + [vmem] * 7,
        out_specs=[anyw] * 4 + [vmem],
        scratch_shapes=[
            pltpu.VMEM((2, 2, 3 * K, 3 * K), F32),
            pltpu.VMEM((2, 2, 3 * K, 3 * K), F32),
            pltpu.VMEM((2, 2, K, K), F32),
            pltpu.VMEM((2, K, K), F32),
            pltpu.VMEM((2 * K, K), BF16),
            pltpu.VMEM((2 * K, K), BF16),
            pltpu.VMEM((K, 2 * K), BF16),
            pltpu.VMEM((K, 2 * K), BF16),
            pltpu.VMEM((2 * K, K), F32),
            pltpu.VMEM((K, 2 * K), F32),
            pltpu.SemaphoreType.DMA((4,)),
        ],
        compiler_params=pltpu.CompilerParams(vmem_limit_bytes=48 << 20),
        cost_estimate=pl.CostEstimate(flops=20_000_000_000, bytes_accessed=24 << 20, transcendentals=0),
        name="frames",
    )(local_at, batch, *pieces, beam, kern, meas, *tables)


def shards(object_field, probe, kernel_phase, measured, positions, batch):
    tile = object_field.shape[2]
    tables = constants()
    phase = even_odd(kernel_phase)
    kern = jnp.stack([jnp.cos(phase), jnp.sin(phase)])
    meas = even_odd(measured)
    corner = jnp.stack([lax.axis_index("tile") * tile, lax.axis_index("slab") * tile])
    local_at = positions - corner[None, :].astype(jnp.int32)
    current, beam = object_field, probe
    for batch_no in range(BATCHES):
        right = shifted(current[..., :K], "slab", -1)
        below = shifted(current[:, :, :K, :], "tile", -1)
        diagonal = shifted(right[:, :, :K, :], "tile", -1)
        g_own, g_right, g_below, g_corner, es = run_batch(
            batch_no, local_at, batch, (current, right, below, diagonal), beam, kern, meas, tables
        )
        peak = jnp.max(beam[0] * beam[0] + beam[1] * beam[1])
        from_above = shifted(g_below, "tile", 1)
        right_above = shifted(g_corner, "tile", 1)
        g_right = g_right + jnp.pad(right_above, ((0, 0), (0, 0), (0, tile - K), (0, 0)))
        from_left = shifted(g_right, "slab", 1)
        total = (
            g_own
            + jnp.pad(from_above, ((0, 0), (0, 0), (0, tile - K), (0, 0)))
            + jnp.pad(from_left, ((0, 0), (0, 0), (0, 0), (0, tile - K)))
        )
        current = current - total / peak
        es = packed_total(es, ("tile", "slab"))
        beam = beam - es[:2] / (es[2] + 1.0)
    return (current, beam)


def solution(mesh):
    in_specs = (
        P(None, None, "tile", "slab"),
        P(),
        P(),
        P(("tile", "slab"), None, None),
        P(("tile", "slab"), None),
        P(("tile", "slab")),
    )
    out_specs = (P(None, None, "tile", "slab"), P())
    return jax.shard_map(shards, mesh=mesh, in_specs=in_specs, out_specs=out_specs, check_vma=False)
```

time: 1110 us -> 563 us (0.51)
  local copies, waits for them, and re-layouts: 258 us -> 23.2 us
  matrix products: 206 us -> 7.32 us
  waiting for transfers between devices: 478 us -> 393 us
  other arithmetic: 90.2 us -> 23.6 us
  Pallas kernels: 0 us -> 49.1 us
  loops' own time: 32.1 us -> 0 us
  starting transfers between devices: 22.2 us -> 50.1 us
    dot_general x96 -> x4, matrix products: 206 us -> 7.32 us  [the longest x2 3.89 us: even_odd(): jnp.einsum('kn,...kc->...nc', pick, value, precision=lax.Precision.HIGHEST)]
    dynamic_update_slice x8 -> x0, local copies, waits for them, and re-layouts: 96.5 us -> none  [place(): return lax.dynamic_update_slice(grads, piece, starts)]
    psum x2, waiting for transfers between devices: 305 us -> 244 us  [packed_total(): return lax.psum(value.reshape(-1), axis).reshape(value.shape)]
    pallas_call x0 -> x2, Pallas kernels: none -> 49.1 us  [run_batch(): pl.pallas_call(functools.partial(batch_kernel, batch_no), out_shape=[jax....]
    gather x28 -> x0, local copies, waits for them, and re-layouts: 41.5 us -> none
    scatter-add x4 -> x0, local copies, waits for them, and re-layouts: 38.6 us -> none  [the longest x2 21.6 us: give_columns(): return kept.at[..., :margin].add(returned)]
    concatenate x7 -> x0, other arithmetic: 35.5 us -> none  [the longest x2 26.7 us: take_rows(): return jnp.concatenate([field, edge], axis=2)]
    another operation x4 -> x0, loops' own time: 32.1 us -> none  [the longest x2 31.5 us: shards(): wide_grads = lax.fori_loop(0, slots, place, jnp.zeros_like(extended))]
  transfers between devices with their start and end apart: 10 -> 14, of which waited for: 8 -> 9; matrix products, arithmetic and copies ran while one was open for 5% -> 6% of each run, Pallas kernels for 0% -> 0%
where the time goes in v1:
time: 563 us; the launch traced here: 561 us
  waiting for transfers between devices  393 us (70%)
  starting transfers between devices  50.1 us (9%)
  Pallas kernels  49.1 us (9%)
  other arithmetic  23.6 us (4%)
  local copies, waits for them, and re-layouts  23.2 us (4%)
  between operations  14.4 us (3%)
  matrix products  7.32 us (1%)
    psum x2, waiting for transfers between devices, packed_total(): return lax.psum(value.reshape(-1), axis).reshape(value.shape)  244 us
    ppermute x12, waiting for transfers between devices, shifted(): lax.ppermute(value, axis, [(source, source + steps) for source in range(f...  149 us
    ppermute x12, starting transfers between devices, shifted(): lax.ppermute(value, axis, [(source, source + steps) for source in range(f...  50 us
    pallas_call x2, Pallas kernels, run_batch(): pl.pallas_call(functools.partial(batch_kernel, batch_no), out_shape=[jax....  49.1 us
    sub x2, other arithmetic, shards(): current = current - total / peak  12.6 us
  transfers between devices with their start and end apart: 14, of which 9 were waited for; matrix products, arithmetic and copies ran while one was open for 6% of the time, Pallas kernels for 0%

profile of v1, /device:TPU:1, one launch (start us, length us, event | category | flops | bytes accessed | tf_op | source)
XLA Modules:
  0.0 561.1 jit_solution(9891876353204231113)
XLA Ops:
  7.2 1.9 slice.86
  9.1 1.4 collective-permute-start
  10.6 1.5 slice.87
  12.1 3.3 collective-permute-start.1
  15.6 1.5 fusion.2
  17.1 41.3 %collective-permute-done.right_ref = f32[2,2,512,256]{3,2,1,0:T(8,128)} collective-permute-done((f32[2,2,512,256]{3,2,1,0:T(8,128)S(1)}, f32[2,2,512,256]{3,2,1,0:T(8,128)}, u32[]{:S(2)}, u32[]{:S(2)}) %collective-permute-start) | collective-permute-done | bytes 2097184 | tf_op jit(solution)/shard_map/ppermute | solution.py:22
  58.4 1.3 slice.102
  59.7 3.5 collective-permute-start.2
  63.2 1.7 cosine_bitcast_fusion
  65.1 1.9 convolution_bitcast_fusion.1
  67.0 2.2 convolution_bitcast_fusion.meas_ref
  69.2 7.8 %collective-permute-done.2.corner_ref = f32[2,2,256,256]{3,2,1,0:T(8,128)S(1)} collective-permute-done((f32[2,2,256,256]{3,2,1,0:T(8,128)S(1)}, f32[2,2,256,256]{3,2,1,0:T(8,128)S(1)}, u32[]{:S(2)}, u32[]{:S(2)}) %collective-permute-start.2) | collective-permute-done | bytes 1048608 | tf_op jit(solution)/shard_map/ppermute | solution.py:22
  77.0 32.8 %frames.2 = (f32[2,2,512,512]{3,2,1,0:T(8,128)}, f32[2,2,512,256]{3,2,1,0:T(8,128)}, f32[2,2,256,512]{3,2,1,0:T(8,128)}, f32[2,2,256,256]{3,2,1,0:T(8,128)S(1)}, f32[3,256,256]{2,1,0:T(8,128)S(1)}) custom-call(s32[4,2]{1,0:T(4,128)S(1)} %broadcast_subtract_fusion.at_ref, s32[4]{0:T(128)S(1)} %copy-done.3, f32[2,2,512,512]{3,2,1,0:T(8,128)} %own_ref.1, ...), custom_call_target="tpu_custom_call" | custom-call | flops 20000000000 | bytes 25165824 | tf_op jit(solution)/shard_map/frames/pallas_call | solution.py:319
  109.8 1.9 collective-permute-start.4
  111.7 1.9 collective-permute-start.3
  113.7 9.8 %collective-permute-done.4 = f32[2,2,256,256]{3,2,1,0:T(8,128)S(1)} collective-permute-done((f32[2,2,256,256]{3,2,1,0:T(8,128)S(1)}, f32[2,2,256,256]{3,2,1,0:T(8,128)S(1)}, u32[]{:S(2)}, u32[]{:S(2)}) %collective-permute-start.4) | collective-permute-done | bytes 1048608 | tf_op jit(solution)/shard_map/ppermute | solution.py:22
  123.5 2.0 pad_add_fusion.1
  125.4 1.6 collective-permute-start.5
  127.7 18.3 %collective-permute-done.3 = f32[2,2,256,512]{3,2,1,0:T(8,128)S(1)} collective-permute-done((f32[2,2,256,512]{3,2,1,0:T(8,128)}, f32[2,2,256,512]{3,2,1,0:T(8,128)S(1)}, u32[]{:S(2)}, u32[]{:S(2)}) %collective-permute-start.3) | collective-permute-done | bytes 2097184 | tf_op jit(solution)/shard_map/ppermute | solution.py:22
  146.0 17.4 %collective-permute-done.5 = f32[2,2,512,256]{3,2,1,0:T(8,128)S(1)} collective-permute-done((f32[2,2,512,256]{3,2,1,0:T(8,128)S(1)}, f32[2,2,512,256]{3,2,1,0:T(8,128)S(1)}, u32[]{:S(2)}, u32[]{:S(2)}) %collective-permute-start.5) | collective-permute-done | bytes 2097184 | tf_op jit(solution)/shard_map/ppermute | solution.py:22
  163.4 4.3 divide_subtract_fusion.1.own_ref
  167.7 1.8 slice.103
  169.5 1.3 collective-permute-start.6
  170.8 1.3 copy.22
  172.1 3.1 slice.104
  175.2 1.9 collective-permute-start.7
  177.1 45.7 %collective-permute-done.6.right_ref = f32[2,2,512,256]{3,2,1,0:T(8,128)} collective-permute-done((f32[2,2,512,256]{3,2,1,0:T(8,128)}, f32[2,2,512,256]{3,2,1,0:T(8,128)}, u32[]{:S(2)}, u32[]{:S(2)}) %collective-permute-start.6) | collective-permute-done | bytes 2097184 | tf_op jit(solution)/shard_map/ppermute | solution.py:22
  222.8 2.3 slice.105
  225.1 1.9 collective-permute-start.8
  227.0 115.0 %all-reduce.9.cloned.1.call-done = f32[196608]{0:T(1024)} async-done(((f32[196608]{0:T(1024)}), f32[196608]{0:T(1024)}) %all-reduce.9.cloned.1.call-update) | async-done | bytes 786448 | tf_op jit(solution)/shard_map/psum | solution.py:26
  342.0 1.7 slice_add_fusion.1
  343.7 1.1 slice.106
  344.9 1.0 add.59
  346.1 1.1 copy-done.5
  347.2 1.1 copy-done.7
  348.3 16.2 %frames.3 = (f32[2,2,512,512]{3,2,1,0:T(8,128)}, f32[2,2,512,256]{3,2,1,0:T(8,128)}, f32[2,2,256,512]{3,2,1,0:T(8,128)}, f32[2,2,256,256]{3,2,1,0:T(8,128)S(1)}, f32[3,256,256]{2,1,0:T(8,128)S(1)}) custom-call(s32[4,2]{1,0:T(4,128)S(1)} %broadcast_subtract_fusion.at_ref, s32[4]{0:T(128)S(1)} %copy-done.3, f32[2,2,512,512]{3,2,1,0:T(8,128)} %copy-done.10, ...), custom_call_target="tpu_custom_call" | custom-call | flops 20000000000 | bytes 25165824 | tf_op jit(solution)/shard_map/frames/pallas_call | solution.py:319
  364.6 27.9 %collective-permute-start.10 = (f32[2,2,256,256]{3,2,1,0:T(8,128)S(1)}, f32[2,2,256,256]{3,2,1,0:T(8,128)S(1)}, u32[]{:S(2)}, u32[]{:S(2)}) collective-permute-start(f32[2,2,256,256]{3,2,1,0:T(8,128)S(1)} %get-tuple-element.20), channel_id=1, source_target_pairs={{0,4},{4,8},{8,12},{12,16},{16,20},{20,24},{24,28},{28,32},{32,36}... | collective-permute-start | bytes 3145736 | tf_op jit(solution)/shard_map/ppermute | solution.py:22
  392.5 1.3 copy.23
  393.8 1.9 collective-permute-start.9
  395.8 8.8 %collective-permute-done.10 = f32[2,2,256,256]{3,2,1,0:T(8,128)S(1)} collective-permute-done((f32[2,2,256,256]{3,2,1,0:T(8,128)S(1)}, f32[2,2,256,256]{3,2,1,0:T(8,128)S(1)}, u32[]{:S(2)}, u32[]{:S(2)}) %collective-permute-start.10) | collective-permute-done | bytes 1048608 | tf_op jit(solution)/shard_map/ppermute | solution.py:22
  404.6 3.2 pad_add_fusion
  407.8 1.4 collective-permute-start.11
  410.0 129.3 %all-reduce.11.cloned.1.call-done = f32[196608]{0:T(1024)} async-done(((f32[196608]{0:T(1024)}), f32[196608]{0:T(1024)}) %all-reduce.11.cloned.1.call-update) | async-done | bytes 786448 | tf_op jit(solution)/shard_map/psum | solution.py:26
  539.3 1.9 slice.110
  541.1 1.2 slice.100
  542.4 1.7 slice_add_fusion
  544.0 1.0 add.65
  545.9 8.3 %divide_subtract_fusion = f32[2,2,512,512]{3,2,1,0:T(8,128)} fusion(f32[2,2,512,512]{3,2,1,0:T(8,128)} %copy-done.10, f32[2,2,512,256]{3,2,1,0:T(8,128)S(1)} %collective-permute-done.11, f32[2,2,512,512]{3,2,1,0:T(8,128)} %get-tuple-element.17, f32[2,2,256,512]{3,2,1,0:T(8,128)} %collective-permute-done.9, f32[]{:T(128)} %fusion.1), kind=kLoop, calls=%fused_computation | loop fusion | flops 4194304 | bytes 16777220 | tf_op jit(solution)/shard_map/sub | solution.py:369
  (48 shorter events, 3.0 us)
Async XLA Ops:
  7.2 57.8 %copy-start = (f32[4,256,256]{2,1,0:T(8,128)S(1)}, f32[4,256,256]{2,1,0:T(8,128)}, u32[]{:S(2)}) copy-start(f32[4,256,256]{2,1,0:T(8,128)} %param.17) | copy-start | bytes 3145732
  7.2 334.8 %all-reduce.9.cloned.1.call-start = ((), (), s32[]{:S(2)}) async-start(), calls=%async_computation | async-start | bytes 1572864 | tf_op jit(solution)/shard_map/psum | solution.py:26
  7.2 3.4 copy-start.11
  9.1 6.3 %copy-start.15 = (s32[4,2]{0,1:T(2,128)S(1)}, s32[4,2]{0,1:T(2,128)}, u32[]{:S(2)}) copy-start(s32[4,2]{0,1:T(2,128)} %param.18) | copy-start | bytes 100
  9.1 6.4 %copy-start.14 = (f32[256,256]{1,0:T(8,128)S(1)}, f32[256,256]{1,0:T(8,128)}, u32[]{:S(2)}) copy-start(f32[256,256]{1,0:T(8,128)} %constant.32.clone) | copy-start | bytes 786436
  9.1 49.3 %collective-permute-start = (f32[2,2,512,256]{3,2,1,0:T(8,128)S(1)}, f32[2,2,512,256]{3,2,1,0:T(8,128)}, u32[]{:S(2)}, u32[]{:S(2)}) collective-permute-start(f32[2,2,512,256]{3,2,1,0:T(8,128)S(1)} %slice.86), channel_id=1, source_target_pairs={{1,0},{2,1},{3,2},{5,4},{6,5},{7,6},{9,8},{10,9},{11,10},{13,12},{... | collective-permute-start | bytes 6291464 | tf_op jit(solution)/shard_map/ppermute | solution.py:22
  12.1 57.1 %collective-permute-start.1 = (f32[2,2,256,512]{3,2,1,0:T(8,128)}, f32[2,2,256,512]{3,2,1,0:T(8,128)}, u32[]{:S(2)}, u32[]{:S(2)}) collective-permute-start(f32[2,2,256,512]{3,2,1,0:T(8,128)} %slice.87), channel_id=1, source_target_pairs={{4,0},{8,4},{12,8},{16,12},{20,16},{24,20},{28,24},{32,28},{36,32}... | collective-permute-start | bytes 6291464 | tf_op jit(solution)/shard_map/ppermute | solution.py:22
  17.1 47.9 %copy-start.13 = (f32[256,256,1]{1,0,2:T(8,128)S(1)}, f32[256,256,1]{1,0,2:T(8,128)}, u32[]{:S(2)}) copy-start(f32[256,256,1]{1,0,2:T(8,128)} %constant.66) | copy-start | bytes 786436
  59.7 17.2 %collective-permute-start.2 = (f32[2,2,256,256]{3,2,1,0:T(8,128)S(1)}, f32[2,2,256,256]{3,2,1,0:T(8,128)S(1)}, u32[]{:S(2)}, u32[]{:S(2)}) collective-permute-start(f32[2,2,256,256]{3,2,1,0:T(8,128)S(1)} %slice.102), channel_id=1, source_target_pairs={{4,0},{8,4},{12,8},{16,12},{20,16},{24,20},{28,24},{32,28},{36,32}... | collective-permute-start | bytes 3145736 | tf_op jit(solution)/shard_map/ppermute | solution.py:22
  65.0 11.9 %copy-start.2 = (f32[2,256,256]{2,1,0:T(8,128)S(1)}, f32[2,256,256]{2,1,0:T(8,128)}, u32[]{:S(2)}) copy-start(f32[2,256,256]{2,1,0:T(8,128)} %beam_ref.1) | copy-start | bytes 1572868
  65.0 11.9 %copy-start.3 = (s32[4]{0:T(128)S(1)}, s32[4]{0:T(128)}, u32[]{:S(2)}) copy-start(s32[4]{0:T(128)} %which_ref.3) | copy-start | bytes 52
  65.0 11.9 %copy-start.4 = (bf16[2,768,256]{2,1,0:T(8,128)(2,1)S(1)}, bf16[2,768,256]{2,1,0:T(8,128)(2,1)}, u32[]{:S(2)}) copy-start(bf16[2,768,256]{2,1,0:T(8,128)(2,1)} %constant.60.mr_ref) | copy-start | bytes 2359300
  65.0 11.9 %copy-start.6 = (bf16[2,256,768]{2,1,0:T(8,128)(2,1)S(1)}, bf16[2,256,768]{2,1,0:T(8,128)(2,1)}, u32[]{:S(2)}) copy-start(bf16[2,256,768]{2,1,0:T(8,128)(2,1)} %constant.65.ml_ref) | copy-start | bytes 2359300
  65.1 11.9 %copy-start.8 = (f32[2,128,128]{2,1,0:T(8,128)S(1)}, f32[2,128,128]{2,1,0:T(8,128)}, u32[]{:S(2)}) copy-start(f32[2,128,128]{2,1,0:T(8,128)} %constant.31.clone.wr_ref) | copy-start | bytes 393220
  65.1 11.9 %copy-start.9 = (f32[2,8,128]{2,1,0:T(8,128)S(1)}, f32[2,8,128]{2,1,0:T(8,128)}, u32[]{:S(2)}) copy-start(f32[2,8,128]{2,1,0:T(8,128)} %constant.30.clone.wl_ref) | copy-start | bytes 24580
  109.8 13.7 %collective-permute-start.4 = (f32[2,2,256,256]{3,2,1,0:T(8,128)S(1)}, f32[2,2,256,256]{3,2,1,0:T(8,128)S(1)}, u32[]{:S(2)}, u32[]{:S(2)}) collective-permute-start(f32[2,2,256,256]{3,2,1,0:T(8,128)S(1)} %get-tuple-element.15), channel_id=1, source_target_pairs={{0,4},{4,8},{8,12},{12,16},{16,20},{20,24},{24,28},{28,32},{32,36}... | collective-permute-start | bytes 3145736 | tf_op jit(solution)/shard_map/ppermute | solution.py:22
  111.7 34.3 %collective-permute-start.3 = (f32[2,2,256,512]{3,2,1,0:T(8,128)}, f32[2,2,256,512]{3,2,1,0:T(8,128)S(1)}, u32[]{:S(2)}, u32[]{:S(2)}) collective-permute-start(f32[2,2,256,512]{3,2,1,0:T(8,128)} %get-tuple-element.13), channel_id=1, source_target_pairs={{0,4},{4,8},{8,12},{12,16},{16,20},{20,24},{24,28},{28,32},{32,36}... | collective-permute-start | bytes 6291464 | tf_op jit(solution)/shard_map/ppermute | solution.py:22
  123.5 39.9 %copy-start.12 = (f32[2,2,512,512]{3,2,1,0:T(8,128)S(1)}, f32[2,2,512,512]{3,2,1,0:T(8,128)}, u32[]{:S(2)}) copy-start(f32[2,2,512,512]{3,2,1,0:T(8,128)} %own_ref.1) | copy-start | bytes 12582916
  125.4 38.0 %collective-permute-start.5 = (f32[2,2,512,256]{3,2,1,0:T(8,128)S(1)}, f32[2,2,512,256]{3,2,1,0:T(8,128)S(1)}, u32[]{:S(2)}, u32[]{:S(2)}) collective-permute-start(f32[2,2,512,256]{3,2,1,0:T(8,128)S(1)} %pad_add_fusion.1), channel_id=1, source_target_pairs={{0,1},{1,2},{2,3},{4,5},{5,6},{6,7},{8,9},{9,10},{10,11},{12,13},{... | collective-permute-start | bytes 6291464 | tf_op jit(solution)/shard_map/ppermute | solution.py:22
  167.7 4.4 copy-start.10
  169.5 53.3 %collective-permute-start.6 = (f32[2,2,512,256]{3,2,1,0:T(8,128)}, f32[2,2,512,256]{3,2,1,0:T(8,128)}, u32[]{:S(2)}, u32[]{:S(2)}) collective-permute-start(f32[2,2,512,256]{3,2,1,0:T(8,128)} %slice.103), channel_id=1, source_target_pairs={{1,0},{2,1},{3,2},{5,4},{6,5},{7,6},{9,8},{10,9},{11,10},{13,12},{... | collective-permute-start | bytes 6291464 | tf_op jit(solution)/shard_map/ppermute | solution.py:22
  172.1 367.2 %all-reduce.11.cloned.1.call-start = ((), (), s32[]{:S(2)}) async-start(), calls=%async_computation.1 | async-start | bytes 1572864 | tf_op jit(solution)/shard_map/psum | solution.py:26
  175.2 170.8 %collective-permute-start.7 = (f32[2,2,256,512]{3,2,1,0:T(8,128)}, f32[2,2,256,512]{3,2,1,0:T(8,128)}, u32[]{:S(2)}, u32[]{:S(2)}) collective-permute-start(f32[2,2,256,512]{3,2,1,0:T(8,128)} %slice.104), channel_id=1, source_target_pairs={{4,0},{8,4},{12,8},{16,12},{20,16},{24,20},{28,24},{32,28},{36,32}... | collective-permute-start | bytes 6291464 | tf_op jit(solution)/shard_map/ppermute | solution.py:22
  225.1 121.0 %collective-permute-start.8 = (f32[2,2,256,256]{3,2,1,0:T(8,128)}, f32[2,2,256,256]{3,2,1,0:T(8,128)S(1)}, u32[]{:S(2)}, u32[]{:S(2)}) collective-permute-start(f32[2,2,256,256]{3,2,1,0:T(8,128)} %slice.105), channel_id=1, source_target_pairs={{4,0},{8,4},{12,8},{16,12},{20,16},{24,20},{28,24},{32,28},{36,32}... | collective-permute-start | bytes 3145736 | tf_op jit(solution)/shard_map/ppermute | solution.py:22
  346.1 1.1 copy-start.5
  347.2 1.1 copy-start.7
  364.6 40.0 %collective-permute-start.10 = (f32[2,2,256,256]{3,2,1,0:T(8,128)S(1)}, f32[2,2,256,256]{3,2,1,0:T(8,128)S(1)}, u32[]{:S(2)}, u32[]{:S(2)}) collective-permute-start(f32[2,2,256,256]{3,2,1,0:T(8,128)S(1)} %get-tuple-element.20), channel_id=1, source_target_pairs={{0,4},{4,8},{8,12},{12,16},{16,20},{20,24},{24,28},{28,32},{32,36}... | collective-permute-start | bytes 3145736 | tf_op jit(solution)/shard_map/ppermute | solution.py:22
  393.8 152.1 %collective-permute-start.9 = (f32[2,2,256,512]{3,2,1,0:T(8,128)}, f32[2,2,256,512]{3,2,1,0:T(8,128)}, u32[]{:S(2)}, u32[]{:S(2)}) collective-permute-start(f32[2,2,256,512]{3,2,1,0:T(8,128)} %get-tuple-element.18), channel_id=1, source_target_pairs={{0,4},{4,8},{8,12},{12,16},{16,20},{20,24},{24,28},{28,32},{32,36}... | collective-permute-start | bytes 6291464 | tf_op jit(solution)/shard_map/ppermute | solution.py:22
  407.8 138.1 %collective-permute-start.11 = (f32[2,2,512,256]{3,2,1,0:T(8,128)}, f32[2,2,512,256]{3,2,1,0:T(8,128)S(1)}, u32[]{:S(2)}, u32[]{:S(2)}) collective-permute-start(f32[2,2,512,256]{3,2,1,0:T(8,128)} %pad_add_fusion), channel_id=1, source_target_pairs={{0,1},{1,2},{2,3},{4,5},{5,6},{6,7},{8,9},{9,10},{10,11},{12,13},{... | collective-permute-start | bytes 6291464 | tf_op jit(solution)/shard_map/ppermute | solution.py:22
  545.9 8.3 %copy-start.1 = (f32[4,256,256]{2,1,0:T(8,128)S(1)}, f32[4,256,256]{2,1,0:T(8,128)}, u32[]{:S(2)}) copy-start(f32[4,256,256]{2,1,0:T(8,128)} %param.17) | copy-start | bytes 3145732
Sparse Core Ops, SparseCore 0:
  172.2 169.7 all-reduce.8
  393.9 145.2 all-reduce.10

commit v2 on v1

--- a/solution.py
+++ b/solution.py
@@ -20,10 +20,6 @@
     count = lax.axis_size(axis)
     first, last = (max(0, -steps), min(count, count - steps))
     return lax.ppermute(value, axis, [(source, source + steps) for source in range(first, last)])
-
-
-def packed_total(value, axis):
-    return lax.psum(value.reshape(-1), axis).reshape(value.shape)
 
 
 def bf16_pair(table):
@@ -227,11 +223,11 @@
             for i in range(0, K, 32):
                 rows = slice(i, i + 32)
                 waves = []
-                for cols in (lo, hi):
-                    br, bi = beam_ref[0, rows, cols], beam_ref[1, rows, cols]
+                for n, cols in enumerate((lo, hi)):
+                    br, bi = beam_ref[0, n, rows, :], beam_ref[1, n, rows, :]
                     pr, pi = patch[0, 0, rows, cols], patch[1, 0, rows, cols]
                     waves += [br * pr - bi * pi, br * pi + bi * pr]
-                    es_ref[2, rows, cols] = es_ref[2, rows, cols] + (pr * pr + pi * pi)
+                    es_ref[2, n, rows, :] = es_ref[2, n, rows, :] + (pr * pr + pi * pi)
                 right_in(i, 32, *waves)
             dot_right(0)
             left_in()
@@ -290,12 +286,12 @@
                 dr, di = [], []
                 for n, cols in enumerate((lo, hi)):
                     gr, gi = gs[2 * n], gs[2 * n + 1]
-                    br, bi = beam_ref[0, rows, cols], beam_ref[1, rows, cols]
+                    br, bi = beam_ref[0, n, rows, :], beam_ref[1, n, rows, :]
                     pr, pi = patch[0, 0, rows, cols], patch[1, 0, rows, cols]
                     dr.append(br * gr + bi * gi)
                     di.append(br * gi - bi * gr)
-                    es_ref[0, rows, cols] = es_ref[0, rows, cols] + (pr * gr + pi * gi)
-                    es_ref[1, rows, cols] = es_ref[1, rows, cols] + (pr * gi - pi * gr)
+                    es_ref[0, n, rows, :] = es_ref[0, n, rows, :] + (pr * gr + pi * gi)
+                    es_ref[1, n, rows, :] = es_ref[1, n, rows, :] + (pr * gi - pi * gr)
                 place(0, i, dr, di)
 
         return carry
@@ -318,7 +314,7 @@
     shapes = [(2, 2, tile, tile), (2, 2, tile, K), (2, 2, K, tile), (2, 2, K, K)]
     return pl.pallas_call(
         functools.partial(batch_kernel, batch_no),
-        out_shape=[jax.ShapeDtypeStruct(s, F32) for s in shapes] + [jax.ShapeDtypeStruct((3, K, K), F32)],
+        out_shape=[jax.ShapeDtypeStruct(s, F32) for s in shapes] + [jax.ShapeDtypeStruct((3, 2, K, HALF), F32)],
         in_specs=[smem, smem] + [anyw] * 4 + [vmem] * 7,
         out_specs=[anyw] * 4 + [vmem],
         scratch_shapes=[
@@ -340,6 +336,277 @@
     )(local_at, batch, *pieces, beam, kern, meas, *tables)
 
 
+MESH = pl.DeviceIdType.MESH
+UNITS = 3 * K * K // (8 * HALF)
+
+
+def exchange_kernel(final, *refs):
+    if final:
+        es, beam, go, gr, gb, gx, ob = refs[:7]
+        beam_new, o_new = refs[7:9]
+        rest = refs[9:]
+    else:
+        es, beam, go, gr, gb, gx, ob, rb = refs[:8]
+        beam_new, o_new, r_new, b_new, x_new = refs[8:13]
+        rest = refs[13:]
+    if final:
+        gov, grv, ov, rx, rbl, from_left, tr = rest[:7]
+        rest = rest[7:]
+    else:
+        gov, grv, ov, rx, rbl, from_left, tr, rv, from_right, tl = rest[:10]
+        rest = rest[10:]
+    scale, rc, acc, rz, acc2, rxs, rys, total, ss, rs, ls = rest
+    t, y = lax.axis_index("tile"), lax.axis_index("slab")
+    tiles, slabs = 32, 4
+    core, x, z = lax.rem(t, 2), lax.rem(t // 2, 4), t // 8
+    partner = (t + 1 - 2 * core, y)
+
+    def zpeer(d):
+        zp = lax.rem(z + d, 4)
+        return zp, ((zp * 4 + x) * 2 + core, y)
+
+    def xpeer(d):
+        xp = lax.rem(x + d, 4)
+        return xp, ((z * 4 + xp) * 2 + core, y)
+
+    def ypeer(d):
+        yp = lax.rem(y + d, 4)
+        return yp, (t, yp)
+
+    under, over = (lax.rem(t + 1, tiles), y), (lax.rem(t + tiles - 1, tiles), y)
+    rightward, leftward = (t, lax.rem(y + 1, slabs)), (t, lax.rem(y + slabs - 1, slabs))
+
+    sent, used = [], [0]
+
+    def send(src, dst, device):
+        n = used[0]
+        used[0] += 1
+        copy = pltpu.make_async_remote_copy(
+            src_ref=src, dst_ref=dst, send_sem=ss.at[n], recv_sem=rs.at[n], device_id=device, device_id_type=MESH
+        )
+        copy.start()
+        sent.append(copy)
+        return copy
+
+    local = [pltpu.make_async_copy(go, gov, ls.at[0]), pltpu.make_async_copy(gr, grv, ls.at[1]), pltpu.make_async_copy(ob, ov, ls.at[2])]
+    if not final:
+        local.append(pltpu.make_async_copy(rb, rv, ls.at[3]))
+    for copy in local:
+        copy.start()
+    barrier = pltpu.get_barrier_semaphore()
+    peers = [partner, under, over] + [p(d)[1] for p in (zpeer, xpeer, ypeer) for d in (1, 2, 3)]
+    for peer in peers:
+        pl.semaphore_signal(barrier, inc=1, device_id=peer, device_id_type=MESH)
+    pl.semaphore_wait(barrier, len(peers))
+
+    def reduce_steps():
+        half, quarter, part = UNITS // 2, UNITS // 8, UNITS // 32
+        copy = send(es.at[pl.ds((1 - core) * half, half)], rc, partner)
+        yield
+        copy.wait_recv()
+        acc[...] = es[pl.ds(core * half, half)] + rc[...]
+        copies = []
+        for d in (1, 2, 3):
+            zp, peer = zpeer(d)
+            copies.append(send(acc.at[pl.ds(zp * quarter, quarter)], rz.at[d - 1], peer))
+        yield
+        for copy in copies:
+            copy.wait_recv()
+        acc2[...] = acc[pl.ds(z * quarter, quarter)] + (rz[0] + rz[1] + rz[2])
+        copies = []
+        for d in (1, 2, 3):
+            xp, peer = xpeer(d)
+            copies.append(send(acc2.at[pl.ds(xp * part, part)], rxs.at[d - 1], peer))
+        yield
+        for copy in copies:
+            copy.wait_recv()
+        rys[y] = acc2[pl.ds(x * part, part)] + (rxs[0] + rxs[1] + rxs[2])
+        copies = [send(rys.at[y], rys.at[y], ypeer(d)[1]) for d in (1, 2, 3)]
+        yield
+        for copy in copies:
+            copy.wait_recv()
+        base = core * half + z * quarter + x * part
+        total[pl.ds(base, part)] = (rys[0] + rys[1]) + (rys[2] + rys[3])
+        for start, size, targets in (
+            (base, part, [xpeer(d)[1] for d in (1, 2, 3)]),
+            (core * half + z * quarter, quarter, [zpeer(d)[1] for d in (1, 2, 3)]),
+            (core * half, half, [partner]),
+        ):
+            piece = total.at[pl.ds(start, size)]
+            copies = [send(piece, piece, peer) for peer in targets]
+            yield
+            for copy in copies:
+                copy.wait_recv()
+        units = UNITS // 3
+        for c in range(2):
+            at = pl.ds(c * units, units)
+            beam_new[at] = beam[at] - total[at] / (total[pl.ds(2 * units, units)] + 1.0)
+
+    top, low = pl.ds(0, K), pl.ds(K, K)
+    first, mid = pl.ds(0, K), pl.ds(K, K)
+
+    def sweep(body):
+        for layer in range(2):
+            def step(i, carry):
+                body(layer, i * 32)
+                return carry
+
+            lax.fori_loop(0, K // 32, step, 0)
+
+    def rows_at(base, i):
+        return pl.ds(pl.multiple_of(base + i, 32), 32)
+
+    def exchange_steps():
+        order = (0, 1)
+        x_corner, x_mid, y_right, y_left, ups, outs = {}, {}, {}, {}, [], []
+
+        def down(c):
+            x_corner[c] = (
+                send(gx.at[c], rx.at[c], under),
+                send(gb.at[c, :, :, first], rbl.at[c, :, :, first], under),
+            )
+
+        def bottom(c):
+            y_right[c] = send(gr.at[c, :, low], from_left.at[c, :, low], rightward)
+            if not final:
+                y_left[c] = send(go.at[c, :, low, first], from_right.at[c, :, low], leftward)
+
+        down(0)
+        bottom(0)
+        yield
+        down(1)
+        yield
+        bottom(1)
+        yield
+        for c in order:
+            x_mid[c] = send(gb.at[c, :, :, mid], rbl.at[c, :, :, mid], under)
+        for copy in local:
+            copy.wait()
+        units = UNITS // 3
+        power = jnp.max(beam[pl.ds(0, units)] ** 2 + beam[pl.ds(units, units)] ** 2, axis=0)
+        peak = jnp.max(jnp.max(power, axis=0, keepdims=True), axis=1, keepdims=True)
+        scale[...] = jnp.broadcast_to(1.0 / peak, (8, K))
+        yield
+        y_right_top, y_left_top = {}, {}
+        for c in order:
+            for copy in x_corner[c]:
+                copy.wait_recv()
+
+            def body(layer, i):
+                at = rows_at(0, i)
+                tr[c, layer, at, :] = grv[c, layer, at, :] + rx[c, layer, at, :]
+                if not final:
+                    tl[c, layer, at, :] = gov[c, layer, at, first] + rbl[c, layer, at, first]
+
+            sweep(body)
+            y_right_top[c] = send(tr.at[c], from_left.at[c, :, top], rightward)
+            if not final:
+                y_left_top[c] = send(tl.at[c], from_right.at[c, :, top], leftward)
+            yield
+        for c in order:
+            x_mid[c].wait_recv()
+
+            def body(layer, i):
+                at, inv = rows_at(0, i), scale[0:1, :]
+                ov[c, layer, at, mid] = ov[c, layer, at, mid] - (gov[c, layer, at, mid] + rbl[c, layer, at, mid]) * inv
+                at = rows_at(K, i)
+                ov[c, layer, at, mid] = ov[c, layer, at, mid] - gov[c, layer, at, mid] * inv
+
+            sweep(body)
+            if not final:
+                ups.append(send(ov.at[c, :, top, mid], b_new.at[c, :, :, mid], over))
+            yield
+        for c in order:
+            y_right[c].wait_recv()
+            if not final:
+                y_left[c].wait_recv()
+
+            def body(layer, i):
+                at, inv = rows_at(K, i), scale[0:1, :]
+                ov[c, layer, at, first] = ov[c, layer, at, first] - (gov[c, layer, at, first] + from_left[c, layer, at, :]) * inv
+                if not final:
+                    rv[c, layer, at, :] = rv[c, layer, at, :] - (grv[c, layer, at, :] + from_right[c, layer, at, :]) * inv
+
+            sweep(body)
+            yield
+        for c in order:
+            y_right_top[c].wait_recv()
+            if not final:
+                y_left_top[c].wait_recv()
+
+            def body(layer, i):
+                at, inv = rows_at(0, i), scale[0:1, :]
+                if final:
+                    own = gov[c, layer, at, first] + rbl[c, layer, at, first]
+                else:
+                    own = tl[c, layer, at, :]
+                    rv[c, layer, at, :] = rv[c, layer, at, :] - (tr[c, layer, at, :] + from_right[c, layer, at, :]) * inv
+                ov[c, layer, at, first] = ov[c, layer, at, first] - (own + from_left[c, layer, at, :]) * inv
+
+            sweep(body)
+            if not final:
+                ups.append(send(ov.at[c, :, top, first], b_new.at[c, :, :, first], over))
+                ups.append(send(rv.at[c, :, top], x_new.at[c], over))
+            outs.append(pltpu.make_async_copy(ov.at[c], o_new.at[c], ls.at[4 + 2 * c]))
+            if not final:
+                outs.append(pltpu.make_async_copy(rv.at[c], r_new.at[c], ls.at[5 + 2 * c]))
+            for copy in outs[-1 if final else -2 :]:
+                copy.start()
+            yield
+        for copy in ups:
+            copy.wait_recv()
+        for copy in outs:
+            copy.wait()
+
+    reduce_run, exchange_run = reduce_steps(), exchange_steps()
+    for turn in "rerrererrereerereeee":
+        next(reduce_run if turn == "r" else exchange_run, None)
+    for run in (exchange_run, reduce_run):
+        for _ in run:
+            pass
+    for copy in sent:
+        copy.wait_send()
+
+
+def run_exchange(final, es, beam, grads, own, right):
+    tile = 2 * K
+    vmem = pl.BlockSpec(memory_space=pltpu.VMEM)
+    anyw = pl.BlockSpec(memory_space=pl.ANY)
+    shape = jax.ShapeDtypeStruct
+    square, strip = pltpu.VMEM((2, 2, tile, tile), F32), pltpu.VMEM((2, 2, tile, K), F32)
+    flat, small = pltpu.VMEM((2, 2, K, tile), F32), pltpu.VMEM((2, 2, K, K), F32)
+    scratch = [square, strip, square, small, flat, strip, small] + ([] if final else [strip, strip, small])
+    scratch += [
+        pltpu.VMEM((8, K), F32),
+        pltpu.VMEM((UNITS // 2, 8, HALF), F32),
+        pltpu.VMEM((UNITS // 2, 8, HALF), F32),
+        pltpu.VMEM((3, UNITS // 8, 8, HALF), F32),
+        pltpu.VMEM((UNITS // 8, 8, HALF), F32),
+        pltpu.VMEM((3, UNITS // 32, 8, HALF), F32),
+        pltpu.VMEM((4, UNITS // 32, 8, HALF), F32),
+        pltpu.VMEM((UNITS, 8, HALF), F32),
+        pltpu.SemaphoreType.DMA((48,)),
+        pltpu.SemaphoreType.DMA((48,)),
+        pltpu.SemaphoreType.DMA((8,)),
+    ]
+    outs = [shape(beam.shape, F32), shape((2, 2, tile, tile), F32)]
+    operands = [es, beam, *grads, own]
+    if not final:
+        outs += [shape((2, 2, tile, K), F32), shape((2, 2, K, tile), F32), shape((2, 2, K, K), F32)]
+        operands.append(right)
+    return pl.pallas_call(
+        functools.partial(exchange_kernel, final),
+        out_shape=outs,
+        in_specs=[vmem, vmem] + [anyw] * (len(operands) - 2),
+        out_specs=[vmem] + [anyw] * (len(outs) - 1),
+        scratch_shapes=scratch,
+        compiler_params=pltpu.CompilerParams(
+            collective_id=1 if final else 0, has_side_effects=True, vmem_limit_bytes=48 << 20
+        ),
+        name="close" if final else "exchange",
+    )(*operands)
+
+
 def shards(object_field, probe, kernel_phase, measured, positions, batch):
     tile = object_field.shape[2]
     tables = constants()
@@ -348,28 +615,21 @@
     meas = even_odd(measured)
     corner = jnp.stack([lax.axis_index("tile") * tile, lax.axis_index("slab") * tile])
     local_at = positions - corner[None, :].astype(jnp.int32)
-    current, beam = object_field, probe
+    beam = probe.reshape(2, K, 2, HALF).transpose(0, 2, 1, 3)
+    own = object_field
+    right = shifted(own[..., :K], "slab", -1)
+    below = shifted(own[:, :, :K, :], "tile", -1)
+    diagonal = shifted(right[:, :, :K, :], "tile", -1)
     for batch_no in range(BATCHES):
-        right = shifted(current[..., :K], "slab", -1)
-        below = shifted(current[:, :, :K, :], "tile", -1)
-        diagonal = shifted(right[:, :, :K, :], "tile", -1)
-        g_own, g_right, g_below, g_corner, es = run_batch(
-            batch_no, local_at, batch, (current, right, below, diagonal), beam, kern, meas, tables
-        )
-        peak = jnp.max(beam[0] * beam[0] + beam[1] * beam[1])
-        from_above = shifted(g_below, "tile", 1)
-        right_above = shifted(g_corner, "tile", 1)
-        g_right = g_right + jnp.pad(right_above, ((0, 0), (0, 0), (0, tile - K), (0, 0)))
-        from_left = shifted(g_right, "slab", 1)
-        total = (
-            g_own
-            + jnp.pad(from_above, ((0, 0), (0, 0), (0, tile - K), (0, 0)))
-            + jnp.pad(from_left, ((0, 0), (0, 0), (0, 0), (0, tile - K)))
-        )
-        current = current - total / peak
-        es = packed_total(es, ("tile", "slab"))
-        beam = beam - es[:2] / (es[2] + 1.0)
-    return (current, beam)
+        *grads, es = run_batch(batch_no, local_at, batch, (own, right, below, diagonal), beam, kern, meas, tables)
+        flat = beam.reshape(UNITS * 2 // 3, 8, HALF)
+        es = es.reshape(UNITS, 8, HALF)
+        if batch_no + 1 < BATCHES:
+            flat, own, right, below, diagonal = run_exchange(False, es, flat, grads, own, right)
+        else:
+            flat, own = run_exchange(True, es, flat, grads, own, None)
+        beam = flat.reshape(2, 2, K, HALF)
+    return (own, beam.transpose(0, 2, 1, 3).reshape(2, K, K))
 
 
 def solution(mesh):

time: 563 us -> 348 us (0.62)
  waiting for transfers between devices: 393 us -> 49.7 us
  Pallas kernels: 49.1 us -> 269 us
  starting transfers between devices: 50.1 us -> 8.31 us
  other arithmetic: 23.6 us -> 0.12 us
  between operations: 14.4 us -> 0.89 us
  local copies, waits for them, and re-layouts: 23.2 us -> 14.9 us
    psum x2 -> x0, waiting for transfers between devices: 244 us -> none  [packed_total(): return lax.psum(value.reshape(-1), axis).reshape(value.shape)]
    pallas_call x0 -> x2, Pallas kernels: none -> 220 us  [run_exchange(): pl.pallas_call(functools.partial(exchange_kernel, final), out_shape=outs,...]
    ppermute x12 -> x3, waiting for transfers between devices: 149 us -> 49.7 us  [shifted(): lax.ppermute(value, axis, [(source, source + steps) for source in range(f...]
    ppermute x12 -> x3, starting transfers between devices: 50 us -> 8.31 us  [shifted(): lax.ppermute(value, axis, [(source, source + steps) for source in range(f...]
    sub x4 -> x0, other arithmetic: 13.6 us -> none  [the longest x2 12.6 us: shards(): current = current - total / peak]
    add x4 -> x0, other arithmetic: 8.55 us -> none  [the longest x2 5.2 us: shards(): g_right + jnp.pad(right_above, ((0, 0), (0, 0), (0, tile - K), (0, 0)))]
    slice x8 -> x2, local copies, waits for them, and re-layouts: 12.5 us -> 4.68 us  [the longest x1 3.2 us: shards(): right = shifted(own[..., :K], 'slab', -1)]
  transfers between devices with their start and end apart: 14 -> 3, of which waited for: 9 -> 2; matrix products, arithmetic and copies ran while one was open for 6% -> 3% of each run, Pallas kernels for 0% -> 0%
where the time goes in v2:
time: 348 us; the launch traced here: 349 us
  Pallas kernels  269 us (77%)
  waiting for transfers between devices  49.7 us (14%)
  local copies, waits for them, and re-layouts  14.9 us (4%)
  starting transfers between devices  8.31 us (2%)
  matrix products  6.36 us (2%)
    pallas_call x2, Pallas kernels, run_exchange(): pl.pallas_call(functools.partial(exchange_kernel, final), out_shape=outs,...  220 us
    ppermute x3, waiting for transfers between devices, shifted(): lax.ppermute(value, axis, [(source, source + steps) for source in range(f...  49.7 us
    pallas_call x2, Pallas kernels, run_batch(): pl.pallas_call(functools.partial(batch_kernel, batch_no), out_shape=[jax....  49.2 us
    ppermute x3, starting transfers between devices, shifted(): lax.ppermute(value, axis, [(source, source + steps) for source in range(f...  8.31 us
    unnamed x31, local copies, waits for them, and re-layouts  7.93 us
  transfers between devices with their start and end apart: 3, of which 2 were waited for; matrix products, arithmetic and copies ran while one was open for 3% of the time, Pallas kernels for 0%

profile of v2, /device:TPU:1, one launch (start us, length us, event | category | flops | bytes accessed | tf_op | source)
XLA Modules:
  0.0 349.4 jit_solution(3681086204490480233)
XLA Ops:
  0.6 0.0 copy-start
  0.6 0.0 copy-start.8
  0.7 3.2 slice.9
  3.9 0.0 copy-start.13
  3.9 1.4 collective-permute-start
  5.3 0.0 copy-done.8
  5.3 1.5 slice.10
  6.8 3.4 collective-permute-start.1
  10.2 0.0 copy-done.13
  10.2 0.1 copy.21
  10.3 0.0 copy-done.11
  10.3 0.2 copy.22
  10.5 0.2 copy.23
  10.7 0.1 pad_add_fusion
  10.8 0.0 copy-done.10
  10.8 0.0 copy-done.12
  10.8 0.6 fusion
  11.4 0.0 copy-start.9
  11.4 41.9 %collective-permute-done.right_ref.refs_7_ = f32[2,2,512,256]{3,2,1,0:T(8,128)} collective-permute-done((f32[2,2,512,256]{3,2,1,0:T(8,128)}, f32[2,2,512,256]{3,2,1,0:T(8,128)}, u32[]{:S(2)}, u32[]{:S(2)}) %collective-permute-start) | collective-permute-done | bytes 2097184 | tf_op jit(solution)/shard_map/ppermute | solution.py:22
  53.3 1.3 slice.12
  54.6 3.5 collective-permute-start.2
  58.1 1.7 cosine_bitcast_fusion
  59.9 0.0 copy-done
  59.9 0.0 copy-done.9
  59.9 0.0 copy-start.3
  59.9 0.0 copy-start.4
  59.9 0.0 copy-start.5
  59.9 0.0 copy-start.6
  60.0 0.0 copy-start.7
  60.0 1.9 convolution_bitcast_fusion.1
  61.9 2.2 convolution_bitcast_fusion.meas_ref
  64.0 0.0 collective-permute-done.1.below_ref
  64.0 7.8 %collective-permute-done.2.corner_ref = f32[2,2,256,256]{3,2,1,0:T(8,128)S(1)} collective-permute-done((f32[2,2,256,256]{3,2,1,0:T(8,128)S(1)}, f32[2,2,256,256]{3,2,1,0:T(8,128)S(1)}, u32[]{:S(2)}, u32[]{:S(2)}) %collective-permute-start.2) | collective-permute-done | bytes 1048608 | tf_op jit(solution)/shard_map/ppermute | solution.py:22
  71.8 0.0 copy-done.3
  71.8 0.0 copy-done.4
  71.8 0.0 copy-done.5
  71.9 0.0 copy-done.6
  71.9 0.0 copy-done.7
  71.9 32.8 %frames.2 = (f32[2,2,512,512]{3,2,1,0:T(8,128)}, f32[2,2,512,256]{3,2,1,0:T(8,128)}, f32[2,2,256,512]{3,2,1,0:T(8,128)}, f32[2,2,256,256]{3,2,1,0:T(8,128)S(1)}, f32[3,2,256,128]{3,2,1,0:T(8,128)S(1)}) custom-call(s32[4,2]{1,0:T(4,128)S(1)} %broadcast_subtract_fusion.at_ref, s32[4]{0:T(128)S(1)} %copy-done.3, f32[2,2,512,512]{3,2,1,0:T(8,128)} %refs_6_.1, ...), custom_call_target="tpu_custom_call" | custom-call | flops 20000000000 | bytes 25165824 | tf_op jit(solution)/shard_map/frames/pallas_call | solution.py:315
  104.6 98.2 %exchange.1 = (f32[128,8,128]{2,1,0:T(8,128)S(1)}, f32[2,2,512,512]{3,2,1,0:T(8,128)}, f32[2,2,512,256]{3,2,1,0:T(8,128)S(1)}, f32[2,2,256,512]{3,2,1,0:T(8,128)}, f32[2,2,256,256]{3,2,1,0:T(8,128)S(1)}) custom-call(f32[192,8,128]{2,1,0:T(8,128)S(1)} %bitcast.40, f32[128,8,128]{2,1,0:T(8,128)S(1)} %bitcast.38, f32[2,2,512,512]{3,2,1,0:T(8,128)} %get-tuple-element.20.refs_2_, ...), custom_call_target="tpu_custom_call" | custom-call | tf_op jit(solution)/shard_map/exchange/pallas_call | solution.py:597
  202.9 0.0 copy-start.2
  202.9 1.3 copy-done.2
  204.2 16.4 %frames.3 = (f32[2,2,512,512]{3,2,1,0:T(8,128)}, f32[2,2,512,256]{3,2,1,0:T(8,128)}, f32[2,2,256,512]{3,2,1,0:T(8,128)}, f32[2,2,256,256]{3,2,1,0:T(8,128)S(1)}, f32[3,2,256,128]{3,2,1,0:T(8,128)S(1)}) custom-call(s32[4,2]{1,0:T(4,128)S(1)} %broadcast_subtract_fusion.at_ref, s32[4]{0:T(128)S(1)} %copy-done.3, ...), custom_call_target="tpu_custom_call" | custom-call | flops 20000000000 | bytes 25165824 | tf_op jit(solution)/shard_map/frames/pallas_call | solution.py:315
  220.7 0.0 copy-start.1
  220.7 1.6 copy-done.1
  222.2 121.6 %close.1 = (f32[128,8,128]{2,1,0:T(8,128)S(1)}, f32[2,2,512,512]{3,2,1,0:T(8,128)}) custom-call(f32[192,8,128]{2,1,0:T(8,128)S(1)} %bitcast.39, f32[128,8,128]{2,1,0:T(8,128)S(1)} %get-tuple-element.28.refs_1_, f32[2,2,512,512]{3,2,1,0:T(8,128)} %get-tuple-element.30.refs_2_, f32[2,2,512,256]{3,2,1,0:T(8,128)S(1)} %copy-done.1, ...), custom_call_target="tpu_custom_call" | custom-call | tf_op jit(solution)/shard_map/close/pallas_call | solution.py:597
  343.9 0.8 copy.32
  344.7 4.6 %copy.34 = f32[2,2,512,512]{3,2,1,0:T(8,128)} copy(f32[2,2,512,512]{3,2,1,0:T(8,128)} %get-tuple-element.40) | data formatting | bytes 8388608
  (5 shorter events, 0.0 us)
Async XLA Ops:
  0.6 59.3 %copy-start = (f32[4,256,256]{2,1,0:T(8,128)S(1)}, f32[4,256,256]{2,1,0:T(8,128)}, u32[]{:S(2)}) copy-start(f32[4,256,256]{2,1,0:T(8,128)} %param.17) | copy-start | bytes 3145732
  0.6 4.6 %copy-start.8 = (f32[2,2,512,512]{3,2,1,0:T(8,128)S(1)}, f32[2,2,512,512]{3,2,1,0:T(8,128)}, u32[]{:S(2)}) copy-start(f32[2,2,512,512]{3,2,1,0:T(8,128)} %refs_6_.1) | copy-start | bytes 12582916
  3.9 6.3 %copy-start.13 = (s32[4,2]{0,1:T(2,128)S(1)}, s32[4,2]{0,1:T(2,128)}, u32[]{:S(2)}) copy-start(s32[4,2]{0,1:T(2,128)} %param.18) | copy-start | bytes 100
  3.9 6.4 %copy-start.11 = (f32[2,256,256]{2,1,0:T(8,128)S(1)}, f32[2,256,256]{2,1,0:T(8,128)}, u32[]{:S(2)}) copy-start(f32[2,256,256]{2,1,0:T(8,128)} %param.15) | copy-start | bytes 1572868
  3.9 49.5 %collective-permute-start = (f32[2,2,512,256]{3,2,1,0:T(8,128)}, f32[2,2,512,256]{3,2,1,0:T(8,128)}, u32[]{:S(2)}, u32[]{:S(2)}) collective-permute-start(f32[2,2,512,256]{3,2,1,0:T(8,128)} %slice.9), channel_id=1, source_target_pairs={{1,0},{2,1},{3,2},{5,4},{6,5},{7,6},{9,8},{10,9},{11,10},{13,12},{... | collective-permute-start | bytes 6291464 | tf_op jit(solution)/shard_map/ppermute | solution.py:22
  6.8 4.0 %copy-start.10 = (f32[256,256]{1,0:T(8,128)S(1)}, f32[256,256]{1,0:T(8,128)}, u32[]{:S(2)}) copy-start(f32[256,256]{1,0:T(8,128)} %constant.25.clone) | copy-start | bytes 786436
  6.8 4.0 %copy-start.12 = (f32[256,256]{1,0:T(8,128)S(1)}, f32[256,256]{1,0:T(8,128)}, u32[]{:S(2)}) copy-start(f32[256,256]{1,0:T(8,128)} %param.16) | copy-start | bytes 786436
  6.8 57.3 %collective-permute-start.1 = (f32[2,2,256,512]{3,2,1,0:T(8,128)}, f32[2,2,256,512]{3,2,1,0:T(8,128)}, u32[]{:S(2)}, u32[]{:S(2)}) collective-permute-start(f32[2,2,256,512]{3,2,1,0:T(8,128)} %slice.10), channel_id=1, source_target_pairs={{4,0},{8,4},{12,8},{16,12},{20,16},{24,20},{28,24},{32,28},{36,32}... | collective-permute-start | bytes 6291464 | tf_op jit(solution)/shard_map/ppermute | solution.py:22
  11.4 48.5 %copy-start.9 = (f32[256,256,1]{1,0,2:T(8,128)S(1)}, f32[256,256,1]{1,0,2:T(8,128)}, u32[]{:S(2)}) copy-start(f32[256,256,1]{1,0,2:T(8,128)} %constant.47) | copy-start | bytes 786436
  54.6 17.2 %collective-permute-start.2 = (f32[2,2,256,256]{3,2,1,0:T(8,128)S(1)}, f32[2,2,256,256]{3,2,1,0:T(8,128)S(1)}, u32[]{:S(2)}, u32[]{:S(2)}) collective-permute-start(f32[2,2,256,256]{3,2,1,0:T(8,128)S(1)} %slice.12), channel_id=1, source_target_pairs={{4,0},{8,4},{12,8},{16,12},{20,16},{24,20},{28,24},{32,28},{36,32}... | collective-permute-start | bytes 3145736 | tf_op jit(solution)/shard_map/ppermute | solution.py:22
  59.9 11.9 %copy-start.3 = (s32[4]{0:T(128)S(1)}, s32[4]{0:T(128)}, u32[]{:S(2)}) copy-start(s32[4]{0:T(128)} %which_ref.3) | copy-start | bytes 52
  59.9 11.9 %copy-start.4 = (bf16[2,256,768]{2,1,0:T(8,128)(2,1)S(1)}, bf16[2,256,768]{2,1,0:T(8,128)(2,1)}, u32[]{:S(2)}) copy-start(bf16[2,256,768]{2,1,0:T(8,128)(2,1)} %constant.46.ml_ref) | copy-start | bytes 2359300
  59.9 11.9 %copy-start.5 = (bf16[2,768,256]{2,1,0:T(8,128)(2,1)S(1)}, bf16[2,768,256]{2,1,0:T(8,128)(2,1)}, u32[]{:S(2)}) copy-start(bf16[2,768,256]{2,1,0:T(8,128)(2,1)} %constant.41.mr_ref) | copy-start | bytes 2359300
  59.9 11.9 %copy-start.6 = (f32[2,128,128]{2,1,0:T(8,128)S(1)}, f32[2,128,128]{2,1,0:T(8,128)}, u32[]{:S(2)}) copy-start(f32[2,128,128]{2,1,0:T(8,128)} %constant.24.clone.wr_ref) | copy-start | bytes 393220
  60.0 11.9 %copy-start.7 = (f32[2,8,128]{2,1,0:T(8,128)S(1)}, f32[2,8,128]{2,1,0:T(8,128)}, u32[]{:S(2)}) copy-start(f32[2,8,128]{2,1,0:T(8,128)} %constant.23.clone.wl_ref) | copy-start | bytes 24580
  202.9 1.3 copy-start.2
  220.7 1.6 copy-start.1

commit v3 on v1

v3 whole, which is shorter than its diff:
```python
import functools
import math

import jax
import jax.numpy as jnp
import numpy as np
from jax import lax
from jax.experimental import pallas as pl
from jax.experimental.pallas import tpu as pltpu
from jax.sharding import PartitionSpec as P

BATCHES = 2
K = 256
HALF = 128
F32 = jnp.float32
BF16 = jnp.bfloat16


def bf16_pair(table):
    table = jnp.asarray(table, F32)
    high = table.astype(BF16)
    low = (table - high.astype(F32)).astype(BF16)
    return high, low


def constants():
    index = np.arange(HALF)
    angle = 2.0 * np.pi * (np.outer(index, index) % HALF) / HALF
    cos, sin = np.cos(angle) / 16.0, -np.sin(angle) / 16.0
    right = np.block([[cos, sin], [-sin, cos]])
    right_inv = np.block([[cos, -sin], [sin, cos]])
    rights, lefts = [], []
    for table in (right, right_inv):
        high, low = bf16_pair(table)
        rights.append(jnp.concatenate([high, low, high], axis=0))
        high, low = bf16_pair(table.T)
        lefts.append(jnp.concatenate([high, low, high], axis=1))
    twist = 2.0 * np.pi * index / K
    wr, wi = np.cos(twist).astype(np.float32), -np.sin(twist).astype(np.float32)
    lanes = jnp.asarray(np.stack([np.broadcast_to(wr, (8, HALF)), np.broadcast_to(wi, (8, HALF))]))
    rows = jnp.asarray(np.stack([np.broadcast_to(wr[:, None], (HALF, HALF)), np.broadcast_to(wi[:, None], (HALF, HALF))]))
    return (jnp.stack(rights), jnp.stack(lefts), lanes, rows)


def even_odd(value):
    order = np.concatenate([np.arange(0, K, 2), np.arange(1, K, 2)])
    pick = np.zeros((K, K), np.float32)
    pick[order, np.arange(K)] = 1.0
    pick = jnp.asarray(pick)
    value = jnp.matmul(value, pick, precision=lax.Precision.HIGHEST)
    return jnp.einsum("kn,...kc->...nc", pick, value, precision=lax.Precision.HIGHEST)


def batch_kernel(
    batch_no, at_ref, which_ref, ext, beam_ref, kern_ref, meas_hbm, mr_ref, ml_ref, wl_ref, wr_ref,
    g_out, es_ref,
    grad, window, meas_ref, patch, quantity, vr, vl, chosen, sems,
):
    count = jnp.int32(0)
    for f in range(which_ref.shape[0]):
        mine = which_ref[f] == batch_no

        @pl.when(mine)
        def _():
            chosen[count] = f

        count = count + mine.astype(jnp.int32)

    def corner_of(f):
        row, col = at_ref[f, 0], at_ref[f, 1]
        return pl.multiple_of((row // 8) * 8, 8), pl.multiple_of((col // HALF) * HALF, HALF)

    def fetches(n):
        f, slot = chosen[n], lax.rem(n, 2)
        row_base, col_base = corner_of(f)
        return (
            pltpu.make_async_copy(
                ext.at[:, :, pl.ds(row_base, K + 8), pl.ds(col_base, K + HALF)], window.at[slot], sems.at[slot]
            ),
            pltpu.make_async_copy(meas_hbm.at[f], meas_ref.at[slot], sems.at[2 + slot]),
        )

    def fetch(n):
        @pl.when(n < count)
        def _():
            for copy in fetches(n):
                copy.start()

    fetch(jnp.int32(0))

    def returns(layer):
        return [pltpu.make_async_copy(grad.at[c, layer], g_out.at[c, layer], sems.at[4 + 2 * c + layer]) for c in range(2)]

    def clear(i, carry):
        rows = pl.ds(pl.multiple_of(i * 64, 64), 64)
        for c in range(2):
            for layer in range(2):
                grad[c, layer, rows, :] = jnp.zeros((64, 3 * K), F32)
        return carry

    lax.fori_loop(0, 12, clear, 0)
    es_ref[...] = jnp.zeros_like(es_ref)

    lane = lax.broadcasted_iota(jnp.int32, (8, HALF), 1)
    sub = lax.broadcasted_iota(jnp.int32, (8, HALF), 0)
    lo, hi = slice(0, HALF), slice(HALF, K)

    def operand(blocks):
        highs = [[block.astype(BF16) for block in row] for row in blocks]
        lows = [
            [(block - high.astype(F32)).astype(BF16) for block, high in zip(row, parts)] for row, parts in zip(blocks, highs)
        ]
        return [jnp.concatenate([jnp.concatenate(row, axis=1) for row in rows], axis=0) for rows in (highs, lows)]

    def dot_right(inverse, cb, blocks):
        high, low = operand(blocks)
        vr[cb] = jnp.dot(jnp.concatenate([high, high, low], axis=1), mr_ref[inverse], preferred_element_type=F32)

    def dot_left(inverse, cb, blocks):
        high, low = operand(blocks)
        vl[cb] = jnp.dot(ml_ref[inverse], jnp.concatenate([high, high, low], axis=0), preferred_element_type=F32)

    def right_in(ar, ai, br, bi):
        wr, wi = wl_ref[0, 0:1, :], wl_ref[1, 0:1, :]
        dr, di = ar - br, ai - bi
        return [ar + br, ai + bi], [dr * wr - di * wi, dr * wi + di * wr]

    def right_out(i, n):
        wr, wi = wl_ref[0, 0:1, :], wl_ref[1, 0:1, :]
        rows = slice(i, i + n)
        er, ei, our, oi = vr[0, rows, lo], vr[0, rows, hi], vr[1, rows, lo], vr[1, rows, hi]
        tr, ti = our * wr + oi * wi, oi * wr - our * wi
        return er + tr, ei + ti, er - tr, ei - ti

    def left_in(cb):
        tops, lows = [], []
        for i in range(0, HALF, 32):
            wr, wi = wr_ref[0, i : i + 32, :], wr_ref[1, i : i + 32, :]
            top, low = slice(i, i + 32), slice(HALF + i, HALF + i + 32)
            ar, ai, br, bi = vr[cb, top, lo], vr[cb, top, hi], vr[cb, low, lo], vr[cb, low, hi]
            dr, di = ar - br, ai - bi
            tops.append([ar + br, dr * wr - di * wi])
            lows.append([ai + bi, dr * wi + di * wr])
        return tops + lows

    def left_out(cb):
        tops, lows = [], []
        for i in range(0, HALF, 32):
            wr, wi = wr_ref[0, i : i + 32, :], wr_ref[1, i : i + 32, :]
            top, low = slice(i, i + 32), slice(HALF + i, HALF + i + 32)
            er, ei, our, oi = vl[cb, top, lo], vl[cb, low, lo], vl[cb, top, hi], vl[cb, low, hi]
            tr, ti = our * wr + oi * wi, oi * wr - our * wi
            tops.append([er + tr, ei + ti])
            lows.append([er - tr, ei - ti])
        return tops + lows

    def at_frequency(change, cb):
        tops, lows = [], []
        for i in range(0, HALF, 32):
            pair = []
            for kb, cols in enumerate((lo, hi)):
                top, low = slice(i, i + 32), slice(HALF + i, HALF + i + 32)
                at = (slice(kb * HALF + i, kb * HALF + i + 32), slice(cb * HALF, cb * HALF + HALF))
                pair.append(change(vl[cb, top, cols], vl[cb, low, cols], at))
            tops.append([pair[0][0], pair[1][0]])
            lows.append([pair[0][1], pair[1][1]])
        return tops + lows

    def both_ways(change, evens, odds):
        dot_right(0, 0, evens)
        dot_right(0, 1, odds)
        for cb in range(2):
            dot_left(0, cb, left_in(cb))
        for cb in range(2):
            dot_left(1, cb, at_frequency(change, cb))
        for cb in range(2):
            dot_right(1, cb, left_out(cb))

    def propagate(re, im, at):
        kr, ki = kern_ref[0][at], kern_ref[1][at]
        return re * kr - im * ki, re * ki + im * kr

    def propagate_back(re, im, at):
        kr, ki = kern_ref[0][at], kern_ref[1][at]
        return re * kr + im * ki, im * kr - re * ki

    def frame(n, carry):
        if n is not None:
            f, slot = chosen[n], lax.rem(n, 2)
            fetch(n + 1)
            for copy in fetches(n):
                copy.wait()
            row, col = at_ref[f, 0], at_ref[f, 1]
            row_base, col_base = corner_of(f)
            down, off = row - row_base, col - col_base
            up, back = lax.rem(8 - down, 8), lax.rem(HALF - off, HALF)
            keep, keep_row = lane < HALF - off, sub < 8 - down
            inside, inside_row = lane >= off, sub >= down
            zero = jnp.zeros((8, HALF), F32)

            def target(i, j):
                return pl.ds(pl.multiple_of(row_base + i, 8), 8), pl.ds(pl.multiple_of(col_base + j * HALF, HALF), HALF)

            def cut(step, carry):
                i = step * 32
                for c in range(2):
                    for layer in range(2):
                        columns = []
                        for j in range(3):
                            turned = [
                                pltpu.roll(
                                    pltpu.roll(
                                        window[slot, c, layer, pl.ds(pl.multiple_of(i + 8 * k, 8), 8), HALF * j : HALF * (j + 1)],
                                        back, 1,
                                    ),
                                    up, 0,
                                )
                                for k in range(5)
                            ]
                            columns.append([jnp.where(keep_row, turned[k], turned[k + 1]) for k in range(4)])
                        for k in range(4):
                            at = pl.ds(pl.multiple_of(i + 8 * k, 8), 8)
                            patch[c, layer, at, lo] = jnp.where(keep, columns[0][k], columns[1][k])
                            patch[c, layer, at, hi] = jnp.where(keep, columns[1][k], columns[2][k])
                return carry

            lax.fori_loop(0, K // 32, cut, 0)

            def place(layer, i, half_r, half_i):
                for c, halves in enumerate((half_r, half_i)):
                    turned = [
                        [pltpu.roll(pltpu.roll(half[8 * k : 8 * k + 8], off, 1), down, 0) for k in range(4)] for half in halves
                    ]
                    left, right = [
                        [
                            jnp.where(inside_row, side[k] if k < 4 else zero, side[k - 1] if k else zero)
                            for k in range(5)
                        ]
                        for side in turned
                    ]
                    for k in range(5):
                        adds = (
                            jnp.where(inside, left[k], zero),
                            jnp.where(inside, right[k], left[k]),
                            jnp.where(inside, zero, right[k]),
                        )
                        for j, add in enumerate(adds):
                            at = (c, layer) + target(i + 8 * k, j)
                            grad[at] = grad[at] + add

            evens, odds = [], []
            for i in range(0, K, 32):
                rows = slice(i, i + 32)
                waves = []
                for n, cols in enumerate((lo, hi)):
                    br, bi = beam_ref[0, n, rows, :], beam_ref[1, n, rows, :]
                    pr, pi = patch[0, 0, rows, cols], patch[1, 0, rows, cols]
                    waves += [br * pr - bi * pi, br * pi + bi * pr]
                    es_ref[2, n, rows, :] = es_ref[2, n, rows, :] + (pr * pr + pi * pi)
                even, odd = right_in(*waves)
                evens.append(even)
                odds.append(odd)
            both_ways(propagate, evens, odds)
            evens, odds = [], []
            for i in range(0, K, 32):
                rows = slice(i, i + 32)
                qs = right_out(i, 32)
                waves = []
                for n, cols in enumerate((lo, hi)):
                    qr, qi = qs[2 * n], qs[2 * n + 1]
                    quantity[0, rows, cols] = qr
                    quantity[1, rows, cols] = qi
                    pr, pi = patch[0, 1, rows, cols], patch[1, 1, rows, cols]
                    waves += [pr * qr - pi * qi, pr * qi + pi * qr]
                even, odd = right_in(*waves)
                evens.append(even)
                odds.append(odd)
            def residual(re, im, at):
                power = re * re + im * im
                factor = 1.0 - meas_ref[slot, at[0], at[1]] * lax.rsqrt(jnp.maximum(power, 0.01))
                return re * factor, im * factor

            both_ways(residual, evens, odds)
            evens, odds = [], []
            for i in range(0, K, 32):
                rows = slice(i, i + 32)
                gs = right_out(i, 32)
                waves, dr, di = [], [], []
                for n, cols in enumerate((lo, hi)):
                    gr, gi = gs[2 * n], gs[2 * n + 1]
                    qr, qi = quantity[0, rows, cols], quantity[1, rows, cols]
                    pr, pi = patch[0, 1, rows, cols], patch[1, 1, rows, cols]
                    dr.append(qr * gr + qi * gi)
                    di.append(qr * gi - qi * gr)
                    waves += [pr * gr + pi * gi, pr * gi - pi * gr]
                even, odd = right_in(*waves)
                evens.append(even)
                odds.append(odd)
                place(1, i, dr, di)

            both_ways(propagate_back, evens, odds)
            evens, odds = [], []
            for i in range(0, K, 32):
                rows = slice(i, i + 32)
                gs = right_out(i, 32)
                dr, di = [], []
                for n, cols in enumerate((lo, hi)):
                    gr, gi = gs[2 * n], gs[2 * n + 1]
                    br, bi = beam_ref[0, n, rows, :], beam_ref[1, n, rows, :]
                    pr, pi = patch[0, 0, rows, cols], patch[1, 0, rows, cols]
                    dr.append(br * gr + bi * gi)
                    di.append(br * gi - bi * gr)
                    es_ref[0, n, rows, :] = es_ref[0, n, rows, :] + (pr * gr + pi * gi)
                    es_ref[1, n, rows, :] = es_ref[1, n, rows, :] + (pr * gi - pi * gr)
                place(0, i, dr, di)

        return carry

    lax.fori_loop(0, count, frame, 0)

    for copy in returns(0) + returns(1):
        copy.start()
    for copy in returns(0) + returns(1):
        copy.wait()


def run_batch(batch_no, local_at, batch, ext, beam, kern, meas, tables):
    smem = pl.BlockSpec(memory_space=pltpu.SMEM)
    vmem = pl.BlockSpec(memory_space=pltpu.VMEM)
    anyw = pl.BlockSpec(memory_space=pl.ANY)
    return pl.pallas_call(
        functools.partial(batch_kernel, batch_no),
        out_shape=[jax.ShapeDtypeStruct((2, 2, 3 * K, 3 * K), F32), jax.ShapeDtypeStruct((3, 2, K, HALF), F32)],
        in_specs=[smem, smem, anyw, vmem, vmem, anyw] + [vmem] * 4,
        out_specs=[anyw, vmem],
        scratch_shapes=[
            pltpu.VMEM((2, 2, 3 * K, 3 * K), F32),
            pltpu.VMEM((2, 2, 2, K + 8, K + HALF), F32),
            pltpu.VMEM((2, K, K), F32),
            pltpu.VMEM((2, 2, K, K), F32),
            pltpu.VMEM((2, K, K), F32),
            pltpu.VMEM((2, K, K), F32),
            pltpu.VMEM((2, K, K), F32),
            pltpu.SMEM((4,), jnp.int32),
            pltpu.SemaphoreType.DMA((8,)),
        ],
        compiler_params=pltpu.CompilerParams(vmem_limit_bytes=48 << 20),
        cost_estimate=pl.CostEstimate(flops=20_000_000_000, bytes_accessed=24 << 20, transcendentals=0),
        name="frames",
    )(local_at, batch, ext, beam, kern, meas, *tables)


MESH = pl.DeviceIdType.MESH
UNITS = 3 * K * K // (8 * HALF)


ORDER = {
    False: "rbrrdbrdbrdbLdtrmttrtmmmMrMMMBBBBTTTTU",
    True: "rdbbrdrbbdLrttdrmmttmrmMrMBrMMBBBTTTTU",
}
PLANES = [(0, 0), (1, 0), (0, 1), (1, 1)]


class Net:
    def __init__(self, send_sems, recv_sems):
        self.t, self.y = t, y = lax.axis_index("tile"), lax.axis_index("slab")
        self.core, self.x, self.z = lax.rem(t, 2), lax.rem(t // 2, 4), t // 8
        self.partner = (t + 1 - 2 * self.core, y)
        self.under, self.over = (lax.rem(t + 1, 32), y), (lax.rem(t + 31, 32), y)
        self.rightward, self.leftward = (t, lax.rem(y + 1, 4)), (t, lax.rem(y + 3, 4))
        self.sems, self.sent = (send_sems, recv_sems), []

    def send(self, src, dst, device):
        n = len(self.sent)
        copy = pltpu.make_async_remote_copy(
            src_ref=src, dst_ref=dst, send_sem=self.sems[0].at[n], recv_sem=self.sems[1].at[n],
            device_id=device, device_id_type=MESH,
        )
        copy.start()
        self.sent.append(copy)
        return copy

    def meet(self, peers):
        barrier = pltpu.get_barrier_semaphore()
        for peer in peers:
            pl.semaphore_signal(barrier, inc=1, device_id=peer, device_id_type=MESH)
        pl.semaphore_wait(barrier, len(peers))

    def finish(self):
        for copy in self.sent:
            copy.wait_send()


def open_kernel(own, ext, held, ss, rs, ls):
    net = Net(ss, rs)
    inward = [pltpu.make_async_copy(own.at[c, layer], held.at[c, layer], ls.at[2 * c + layer]) for c, layer in PLANES]
    for copy in inward:
        copy.start()
    net.meet([net.over, net.under, net.leftward, net.rightward])
    top, low, first = pl.ds(0, K), pl.ds(K, K), pl.ds(0, K)
    outer = pl.ds(2 * K, K)
    tops = [net.send(own.at[p + (top, first)], ext.at[p + (top, outer)], net.leftward) for p in PLANES]
    belows = [net.send(own.at[p + (top,)], ext.at[p + (outer, pl.ds(0, 2 * K))], net.over) for p in PLANES]
    lows = [net.send(own.at[p + (low, first)], ext.at[p + (low, outer)], net.leftward) for p in PLANES]
    for copy in inward:
        copy.wait()
    outward = [
        pltpu.make_async_copy(held.at[p], ext.at[p + (pl.ds(0, 2 * K), pl.ds(0, 2 * K))], ls.at[2 * p[0] + p[1]]) for p in PLANES
    ]
    for copy in outward:
        copy.start()
    corners = []
    for p, copy in zip(PLANES, tops):
        copy.wait_recv()
        corners.append(net.send(ext.at[p + (top, outer)], ext.at[p + (outer, outer)], net.over))
    for copy in belows + lows + corners:
        copy.wait_recv()
    for copy in outward:
        copy.wait()
    net.finish()


def run_open(own):
    anyw = pl.BlockSpec(memory_space=pl.ANY)
    return pl.pallas_call(
        open_kernel,
        out_shape=jax.ShapeDtypeStruct((2, 2, 3 * K, 3 * K), F32),
        in_specs=[anyw],
        out_specs=anyw,
        scratch_shapes=[
            pltpu.VMEM((2, 2, 2 * K, 2 * K), F32),
            pltpu.SemaphoreType.DMA((16,)),
            pltpu.SemaphoreType.DMA((16,)),
            pltpu.SemaphoreType.DMA((4,)),
        ],
        compiler_params=pltpu.CompilerParams(collective_id=2, has_side_effects=True, vmem_limit_bytes=48 << 20),
        name="open",
    )(own)


def exchange_kernel(final, *refs):
    es, beam, g, ext, beam_new, new = refs[:6]
    gov, grv, ov, rx, rbl, from_left, tr = refs[6:13]
    rest = refs[13:]
    if not final:
        rv, from_right, tl = rest[:3]
        rest = rest[3:]
    scale, rc, acc, rz, acc2, rxs, rys, total, ss, rs, ls = rest
    net = Net(ss, rs)
    core, x, y, z, partner, send = net.core, net.x, net.y, net.z, net.partner, net.send
    under, over, rightward, leftward = net.under, net.over, net.rightward, net.leftward

    def zpeer(d):
        zp = lax.rem(z + d, 4)
        return zp, ((zp * 4 + x) * 2 + core, y)

    def xpeer(d):
        xp = lax.rem(x + d, 4)
        return xp, ((z * 4 + xp) * 2 + core, y)

    def ypeer(d):
        yp = lax.rem(y + d, 4)
        return yp, (net.t, yp)

    whole, outer = pl.ds(0, 2 * K), pl.ds(2 * K, K)
    square, strip = (slice(None), slice(None), whole, whole), (slice(None), slice(None), whole, outer)
    local = [
        pltpu.make_async_copy(g.at[square], gov, ls.at[0]),
        pltpu.make_async_copy(g.at[strip], grv, ls.at[1]),
        pltpu.make_async_copy(ext.at[square], ov, ls.at[2]),
    ]
    if not final:
        local.append(pltpu.make_async_copy(ext.at[strip], rv, ls.at[3]))
    for copy in local:
        copy.start()
    net.meet([partner, under, over] + [p(d)[1] for p in (zpeer, xpeer, ypeer) for d in (1, 2, 3)])

    def reduce_steps():
        half, quarter, part = UNITS // 2, UNITS // 8, UNITS // 32
        copy = send(es.at[pl.ds((1 - core) * half, half)], rc, partner)
        yield
        copy.wait_recv()
        acc[...] = es[pl.ds(core * half, half)] + rc[...]
        copies = []
        for d in (1, 2, 3):
            zp, peer = zpeer(d)
            copies.append(send(acc.at[pl.ds(zp * quarter, quarter)], rz.at[d - 1], peer))
        yield
        for copy in copies:
            copy.wait_recv()
        acc2[...] = acc[pl.ds(z * quarter, quarter)] + (rz[0] + rz[1] + rz[2])
        copies = []
        for d in (1, 2, 3):
            xp, peer = xpeer(d)
            copies.append(send(acc2.at[pl.ds(xp * part, part)], rxs.at[d - 1], peer))
        yield
        for copy in copies:
            copy.wait_recv()
        rys[y] = acc2[pl.ds(x * part, part)] + (rxs[0] + rxs[1] + rxs[2])
        copies = [send(rys.at[y], rys.at[y], ypeer(d)[1]) for d in (1, 2, 3)]
        yield
        for copy in copies:
            copy.wait_recv()
        base = core * half + z * quarter + x * part
        total[pl.ds(base, part)] = (rys[0] + rys[1]) + (rys[2] + rys[3])
        for start, size, targets in (
            (base, part, [xpeer(d)[1] for d in (1, 2, 3)]),
            (core * half + z * quarter, quarter, [zpeer(d)[1] for d in (1, 2, 3)]),
            (core * half, half, [partner]),
        ):
            piece = total.at[pl.ds(start, size)]
            copies = [send(piece, piece, peer) for peer in targets]
            yield
            for copy in copies:
                copy.wait_recv()
        units = UNITS // 3
        for c in range(2):
            at = pl.ds(c * units, units)
            beam_new[at] = beam[at] - total[at] / (total[pl.ds(2 * units, units)] + 1.0)

    top, low = pl.ds(0, K), pl.ds(K, K)
    first, mid = pl.ds(0, K), pl.ds(K, K)

    def sweep(body):
        def step(i, carry):
            body(i * 32)
            return carry

        lax.fori_loop(0, K // 32, step, 0)

    def rows_at(base, i):
        return pl.ds(pl.multiple_of(base + i, 32), 32)

    corners, mids, lows, tops, ups, outs = {}, {}, {}, {}, [], []

    def down(p):
        corners[p] = (
            send(g.at[p + (outer, outer)], rx.at[p], under),
            send(g.at[p + (outer, first)], rbl.at[p + (slice(None), first)], under),
        )

    def bottom(p):
        lows[p] = [send(g.at[p + (low, outer)], from_left.at[p + (low,)], rightward)]
        if not final:
            lows[p].append(send(g.at[p + (low, first)], from_right.at[p + (low,)], leftward))

    def middle(p):
        mids[p] = send(g.at[p + (outer, mid)], rbl.at[p + (slice(None), mid)], under)

    def ready(_):
        for copy in local:
            copy.wait()
        units = UNITS // 3
        power = jnp.max(beam[pl.ds(0, units)] ** 2 + beam[pl.ds(units, units)] ** 2, axis=0)
        peak = jnp.max(jnp.max(power, axis=0, keepdims=True), axis=1, keepdims=True)
        scale[...] = jnp.broadcast_to(1.0 / peak, (8, K))

    def send_top(p):
        for copy in corners[p]:
            copy.wait_recv()

        def body(i):
            at = p + (rows_at(0, i),)
            tr[at] = grv[at] + rx[at]
            if not final:
                tl[at] = gov[at + (first,)] + rbl[at + (first,)]

        sweep(body)
        tops[p] = [send(tr.at[p], from_left.at[p + (top,)], rightward)]
        if not final:
            tops[p].append(send(tl.at[p], from_right.at[p + (top,)], leftward))

    def use_middle(p):
        mids[p].wait_recv()

        def body(i):
            inv = scale[0:1, :]
            at = p + (rows_at(0, i), mid)
            ov[at] = ov[at] - (gov[at] + rbl[at]) * inv
            at = p + (rows_at(K, i), mid)
            ov[at] = ov[at] - gov[at] * inv

        sweep(body)
        if not final:
            ups.append(send(ov.at[p + (top, mid)], new.at[p + (outer, mid)], over))

    def use_bottom(p):
        for copy in lows[p]:
            copy.wait_recv()

        def body(i):
            inv, at = scale[0:1, :], p + (rows_at(K, i),)
            ov[at + (first,)] = ov[at + (first,)] - (gov[at + (first,)] + from_left[at]) * inv
            if not final:
                rv[at] = rv[at] - (grv[at] + from_right[at]) * inv

        sweep(body)

    def use_top(p):
        for copy in tops[p]:
            copy.wait_recv()

        def body(i):
            inv, at = scale[0:1, :], p + (rows_at(0, i),)
            if final:
                mine = gov[at + (first,)] + rbl[at + (first,)]
            else:
                mine = tl[at]
                rv[at] = rv[at] - (tr[at] + from_right[at]) * inv
            ov[at + (first,)] = ov[at + (first,)] - (mine + from_left[at]) * inv

        sweep(body)
        n = len(outs)
        outs.append(pltpu.make_async_copy(ov.at[p], new.at[p + (whole, whole)], ls.at[4 + n]))
        if not final:
            ups.append(send(ov.at[p + (top, first)], new.at[p + (outer, first)], over))
            ups.append(send(rv.at[p + (top,)], new.at[p + (outer, outer)], over))
            outs.append(pltpu.make_async_copy(rv.at[p], new.at[p + (whole, outer)], ls.at[5 + n]))
        for copy in outs[n:]:
            copy.start()

    def settle(_):
        for copy in ups:
            copy.wait_recv()
        for copy in outs:
            copy.wait()

    reduce_run = reduce_steps()
    acts = {"d": down, "b": bottom, "m": middle, "L": ready, "t": send_top, "M": use_middle, "B": use_bottom, "T": use_top, "U": settle}
    done = {}
    for turn in ORDER[final]:
        if turn == "r":
            next(reduce_run, None)
        else:
            done[turn] = done.get(turn, -1) + 1
            acts[turn](PLANES[done[turn]])
    for _ in reduce_run:
        pass
    net.finish()


def run_exchange(final, es, beam, grads, ext):
    tile = 2 * K
    vmem = pl.BlockSpec(memory_space=pltpu.VMEM)
    anyw = pl.BlockSpec(memory_space=pl.ANY)
    shape = jax.ShapeDtypeStruct
    square, strip = pltpu.VMEM((2, 2, tile, tile), F32), pltpu.VMEM((2, 2, tile, K), F32)
    flat, small = pltpu.VMEM((2, 2, K, tile), F32), pltpu.VMEM((2, 2, K, K), F32)
    scratch = [square, strip, square, small, flat, strip, small] + ([] if final else [strip, strip, small])
    scratch += [
        pltpu.VMEM((8, K), F32),
        pltpu.VMEM((UNITS // 2, 8, HALF), F32),
        pltpu.VMEM((UNITS // 2, 8, HALF), F32),
        pltpu.VMEM((3, UNITS // 8, 8, HALF), F32),
        pltpu.VMEM((UNITS // 8, 8, HALF), F32),
        pltpu.VMEM((3, UNITS // 32, 8, HALF), F32),
        pltpu.VMEM((4, UNITS // 32, 8, HALF), F32),
        pltpu.VMEM((UNITS, 8, HALF), F32),
        pltpu.SemaphoreType.DMA((64,)),
        pltpu.SemaphoreType.DMA((64,)),
        pltpu.SemaphoreType.DMA((12,)),
    ]
    edge = tile if final else 3 * K
    return pl.pallas_call(
        functools.partial(exchange_kernel, final),
        out_shape=[shape(beam.shape, F32), shape((2, 2, edge, edge), F32)],
        in_specs=[vmem, vmem, anyw, anyw],
        out_specs=[vmem, anyw],
        scratch_shapes=scratch,
        compiler_params=pltpu.CompilerParams(
            collective_id=1 if final else 0, has_side_effects=True, vmem_limit_bytes=48 << 20
        ),
        name="close" if final else "exchange",
    )(es, beam, grads, ext)


def shards(object_field, probe, kernel_phase, measured, positions, batch):
    tile = object_field.shape[2]
    tables = constants()
    phase = even_odd(kernel_phase)
    kern = jnp.stack([jnp.cos(phase), jnp.sin(phase)])
    meas = even_odd(measured)
    corner = jnp.stack([lax.axis_index("tile") * tile, lax.axis_index("slab") * tile])
    local_at = positions - corner[None, :].astype(jnp.int32)
    beam = probe.reshape(2, K, 2, HALF).transpose(0, 2, 1, 3)
    ext = run_open(object_field)
    for batch_no in range(BATCHES):
        grads, es = run_batch(batch_no, local_at, batch, ext, beam, kern, meas, tables)
        flat, ext = run_exchange(
            batch_no + 1 == BATCHES, es.reshape(UNITS, 8, HALF), beam.reshape(UNITS * 2 // 3, 8, HALF), grads, ext
        )
        beam = flat.reshape(2, 2, K, HALF)
    return (ext, beam.transpose(0, 2, 1, 3).reshape(2, K, K))


def solution(mesh):
    in_specs = (
        P(None, None, "tile", "slab"),
        P(),
        P(),
        P(("tile", "slab"), None, None),
        P(("tile", "slab"), None),
        P(("tile", "slab")),
    )
    out_specs = (P(None, None, "tile", "slab"), P())
    return jax.shard_map(shards, mesh=mesh, in_specs=in_specs, out_specs=out_specs, check_vma=False)
```

time: 563 us -> 288 us (0.51)
  waiting for transfers between devices: 393 us -> 0 us
  Pallas kernels: 49.1 us -> 269 us
  starting transfers between devices: 50.1 us -> 0 us
  other arithmetic: 23.6 us -> 0.12 us
  local copies, waits for them, and re-layouts: 23.2 us -> 7.34 us
  between operations: 14.4 us -> 0.84 us
    psum x2 -> x0, waiting for transfers between devices: 244 us -> none  [packed_total(): return lax.psum(value.reshape(-1), axis).reshape(value.shape)]
    pallas_call x0 -> x3, Pallas kernels: none -> 231 us  [the longest x2 185 us: run_exchange(): pl.pallas_call(functools.partial(exchange_kernel, final), out_shape=[shap...]
    ppermute x12 -> x0, waiting for transfers between devices: 149 us -> none  [shifted(): lax.ppermute(value, axis, [(source, source + steps) for source in range(f...]
    ppermute x12 -> x0, starting transfers between devices: 50 us -> none  [shifted(): lax.ppermute(value, axis, [(source, source + steps) for source in range(f...]
    slice x10 -> x0, local copies, waits for them, and re-layouts: 16.1 us -> none  [the longest x2 4.59 us: shards(): below = shifted(current[:, :, :K, :], 'tile', -1)]
    sub x4 -> x0, other arithmetic: 13.6 us -> none  [the longest x2 12.6 us: shards(): current = current - total / peak]
    pallas_call x2, Pallas kernels: 49.1 us -> 37.5 us  [run_batch(): pl.pallas_call(functools.partial(batch_kernel, batch_no), out_shape=[jax....]
    add x4 -> x0, other arithmetic: 8.55 us -> none  [the longest x2 5.2 us: shards(): g_right + jnp.pad(right_above, ((0, 0), (0, 0), (0, tile - K), (0, 0)))]
  transfers between devices with their start and end apart: 14 -> 0, of which waited for: 9 -> 0; matrix products, arithmetic and copies ran while one was open for 6% -> 0% of each run, Pallas kernels for 0% -> 0%
where the time goes in v3:
time: 288 us; the launch traced here: 286 us
  Pallas kernels  269 us (93%)
  matrix products  9.18 us (3%)
  local copies, waits for them, and re-layouts  7.34 us (3%)
    pallas_call x2, Pallas kernels, run_exchange(): pl.pallas_call(functools.partial(exchange_kernel, final), out_shape=[shap...  185 us
    pallas_call x1, Pallas kernels, run_open(): pl.pallas_call(open_kernel, out_shape=jax.ShapeDtypeStruct((2, 2, 3 * K,...  46.1 us
    pallas_call x2, Pallas kernels, run_batch(): pl.pallas_call(functools.partial(batch_kernel, batch_no), out_shape=[jax....  37.5 us
    unnamed x17, local copies, waits for them, and re-layouts  6.31 us

profile of v3, /device:TPU:1, one launch (start us, length us, event | category | flops | bytes accessed | tf_op | source)
XLA Modules:
  0.0 286.4 jit_solution(8657455445991490434)
XLA Ops:
  0.6 0.0 copy-start
  0.7 0.1 pad_add_fusion
  0.7 0.8 copy.21
  1.6 1.6 fusion
  3.2 2.6 cosine_bitcast_fusion
  5.9 1.2 copy.22
  7.1 0.2 copy.23
  7.3 0.0 copy-start.2
  7.3 0.0 copy-start.3
  7.3 0.0 copy-start.4
  7.3 0.0 copy-start.5
  7.4 0.0 copy-start.6
  7.4 0.0 copy-done
  7.4 2.9 %convolution_bitcast_fusion.1 = f32[4,256,256]{1,2,0:T(8,128)S(1)} fusion(f32[256,256,1]{1,0,2:T(8,128)} %constant.47, f32[4,256,256]{2,1,0:T(8,128)S(1)} %copy-done), kind=kOutput, calls=%fused_computation.1 | convolution fusion | flops 805306368 | bytes 2359296 | tf_op jit(solution)/shard_map/dot_general | solution.py:50
  10.3 2.0 convolution_bitcast_fusion.meas_hbm
  12.3 0.0 copy-start.1
  12.4 2.2 copy-done.1
  14.5 46.1 %open.1.ext.refs_3_ = f32[2,2,768,768]{3,2,1,0:T(8,128)} custom-call(f32[2,2,512,512]{3,2,1,0:T(8,128)S(1)} %copy-done.1), custom_call_target="tpu_custom_call" | custom-call | tf_op jit(solution)/shard_map/open/pallas_call | solution.py:425
  60.6 0.0 copy-done.2
  60.6 0.0 copy-done.3
  60.6 0.0 copy-done.4
  60.6 0.0 copy-done.5
  60.6 0.0 copy-done.6
  60.7 18.7 %frames.2 = (f32[2,2,768,768]{3,2,1,0:T(8,128)}, f32[3,2,256,128]{3,2,1,0:T(8,128)S(1)}) custom-call(s32[4,2]{1,0:T(4,128)S(1)} %broadcast_subtract_fusion.at_ref, s32[4]{0:T(128)S(1)} %copy-done.2, f32[2,2,768,768]{3,2,1,0:T(8,128)} %open.1.ext.refs_3_, f32[2,2,256,128]{3,2,1,0:T(8,128)S(1)} %bitcast.37, f32[2,256,256]{2,1,0:T(8,128)S(1)} %pad_maximum_fusion.kern_ref, ...), custom_call_target="tpu_custom_call" | custom-call | flops 20000000000 | bytes 25165824 | tf_op jit(solution)/shard_map/frames/pallas_call | solution.py:331
  79.4 110.6 %exchange.1 = (f32[128,8,128]{2,1,0:T(8,128)S(1)}, f32[2,2,768,768]{3,2,1,0:T(8,128)}) custom-call(f32[192,8,128]{2,1,0:T(8,128)S(1)} %bitcast.40, f32[128,8,128]{2,1,0:T(8,128)S(1)} %bitcast.38, f32[2,2,768,768]{3,2,1,0:T(8,128)} %get-tuple-element.11.refs_2_, f32[2,2,768,768]{3,2,1,0:T(8,128)} %open.1.ext.refs_3_), custom_call_target="tpu_custom_call" | custom-call | tf_op jit(solution)/shard_map/exchange/pallas_call | solution.py:664
  190.0 18.8 %frames.3 = (f32[2,2,768,768]{3,2,1,0:T(8,128)}, f32[3,2,256,128]{3,2,1,0:T(8,128)S(1)}) custom-call(s32[4,2]{1,0:T(4,128)S(1)} %broadcast_subtract_fusion.at_ref, s32[4]{0:T(128)S(1)} %copy-done.2, f32[2,2,768,768]{3,2,1,0:T(8,128)} %get-tuple-element.12.ext.refs_3_, f32[2,2,256,128]{3,2,1,0:T(8,128)S(1)} %bitcast.41, ...), custom_call_target="tpu_custom_call" | custom-call | flops 20000000000 | bytes 25165824 | tf_op jit(solution)/shard_map/frames/pallas_call | solution.py:331
  208.8 74.8 %close.1 = (f32[128,8,128]{2,1,0:T(8,128)S(1)}, f32[2,2,512,512]{3,2,1,0:T(8,128)S(1)}) custom-call(f32[192,8,128]{2,1,0:T(8,128)S(1)} %bitcast.39, f32[128,8,128]{2,1,0:T(8,128)S(1)} %get-tuple-element.13.refs_1_, f32[2,2,768,768]{3,2,1,0:T(8,128)} %get-tuple-element.15.refs_2_, f32[2,2,768,768]{3,2,1,0:T(8,128)} %get-tuple-element.12.ext.refs_3_), custom_call_target="tpu_custom_call" | custom-call | tf_op jit(solution)/shard_map/close/pallas_call | solution.py:664
  283.6 0.8 copy.32
  284.4 2.0 copy.34
  (2 shorter events, 0.0 us)
Async XLA Ops:
  0.6 6.7 %copy-start = (f32[4,256,256]{2,1,0:T(8,128)S(1)}, f32[4,256,256]{2,1,0:T(8,128)}, u32[]{:S(2)}) copy-start(f32[4,256,256]{2,1,0:T(8,128)} %param.17) | copy-start | bytes 3145732
  7.3 53.3 %copy-start.2 = (s32[4]{0:T(128)S(1)}, s32[4]{0:T(128)}, u32[]{:S(2)}) copy-start(s32[4]{0:T(128)} %which_ref.3) | copy-start | bytes 52
  7.3 53.3 %copy-start.3 = (bf16[2,256,768]{2,1,0:T(8,128)(2,1)S(1)}, bf16[2,256,768]{2,1,0:T(8,128)(2,1)}, u32[]{:S(2)}) copy-start(bf16[2,256,768]{2,1,0:T(8,128)(2,1)} %constant.46.ml_ref) | copy-start | bytes 2359300
  7.3 53.3 %copy-start.4 = (bf16[2,768,256]{2,1,0:T(8,128)(2,1)S(1)}, bf16[2,768,256]{2,1,0:T(8,128)(2,1)}, u32[]{:S(2)}) copy-start(bf16[2,768,256]{2,1,0:T(8,128)(2,1)} %constant.41.mr_ref) | copy-start | bytes 2359300
  7.3 53.3 %copy-start.5 = (f32[2,128,128]{2,1,0:T(8,128)S(1)}, f32[2,128,128]{2,1,0:T(8,128)}, u32[]{:S(2)}) copy-start(f32[2,128,128]{2,1,0:T(8,128)} %constant.24.clone.wr_ref) | copy-start | bytes 393220
  7.4 53.3 %copy-start.6 = (f32[2,8,128]{2,1,0:T(8,128)S(1)}, f32[2,8,128]{2,1,0:T(8,128)}, u32[]{:S(2)}) copy-start(f32[2,8,128]{2,1,0:T(8,128)} %constant.23.clone.wl_ref) | copy-start | bytes 24580
  12.3 2.2 copy-start.1

commit v4 on v3

--- a/solution.py
+++ b/solution.py
@@ -42,13 +42,25 @@
     return (jnp.stack(rights), jnp.stack(lefts), lanes, rows)
 
 
-def even_odd(value):
+def even_odd_table():
     order = np.concatenate([np.arange(0, K, 2), np.arange(1, K, 2)])
     pick = np.zeros((K, K), np.float32)
-    pick[order, np.arange(K)] = 1.0
-    pick = jnp.asarray(pick)
-    value = jnp.matmul(value, pick, precision=lax.Precision.HIGHEST)
-    return jnp.einsum("kn,...kc->...nc", pick, value, precision=lax.Precision.HIGHEST)
+    pick[np.arange(K), order] = 1.0
+    return jnp.asarray(np.stack([pick, pick.T]), BF16)
+
+
+def three_parts(value):
+    parts = []
+    for _ in range(3):
+        part = value.astype(BF16)
+        parts.append(part)
+        value = value - part.astype(F32)
+    return parts
+
+
+def even_odd(value, pick_ref):
+    moved = sum(jnp.dot(pick_ref[0], part, preferred_element_type=F32) for part in three_parts(value))
+    return sum(jnp.dot(part, pick_ref[1], preferred_element_type=F32) for part in three_parts(moved))
 
 
 def batch_kernel(
@@ -356,7 +368,7 @@
 
 ORDER = {
     False: "rbrrdbrdbrdbLdtrmttrtmmmMrMMMBBBBTTTTU",
-    True: "rdbbrdrbbdLrttdrmmttmrmMrMBrMMBBBTTTTU",
+    True: "rsbrrdfrbdrdLfrtdtfmtmfrtmmMMMrMBBTTBBTTU",
 }
 PLANES = [(0, 0), (1, 0), (0, 1), (1, 1)]
 
@@ -391,7 +403,25 @@
             copy.wait_send()
 
 
-def open_kernel(own, ext, held, ss, rs, ls):
+LONG = 2
+
+
+class Relay:
+    def __init__(self, net, first, second, device, pieces):
+        self.net, self.device, self.ways = net, device, (first, second)
+        self.targets = [target for _, target in pieces]
+        self.hops = [net.send(source, first.at[k], device) for k, (source, _) in enumerate(pieces)]
+        self.at = 0
+
+    def forward(self):
+        stage, k = divmod(self.at, len(self.targets))
+        self.at += 1
+        self.hops[k].wait_recv()
+        target = self.ways[1].at[k] if stage == 0 else self.targets[k]
+        self.hops[k] = self.net.send(self.ways[stage].at[k], target, self.device)
+
+
+def open_kernel(own, phase, meas, pick, ext, kern_out, meas_out, held, way1, way2, ss, rs, ls):
     net = Net(ss, rs)
     inward = [pltpu.make_async_copy(own.at[c, layer], held.at[c, layer], ls.at[2 * c + layer]) for c, layer in PLANES]
     for copy in inward:
@@ -399,9 +429,10 @@
     net.meet([net.over, net.under, net.leftward, net.rightward])
     top, low, first = pl.ds(0, K), pl.ds(K, K), pl.ds(0, K)
     outer = pl.ds(2 * K, K)
+    relay = Relay(net, way1, way2, net.rightward, [(own.at[p + (low, first)], ext.at[p + (low, outer)]) for p in PLANES[:LONG]])
     tops = [net.send(own.at[p + (top, first)], ext.at[p + (top, outer)], net.leftward) for p in PLANES]
     belows = [net.send(own.at[p + (top,)], ext.at[p + (outer, pl.ds(0, 2 * K))], net.over) for p in PLANES]
-    lows = [net.send(own.at[p + (low, first)], ext.at[p + (low, outer)], net.leftward) for p in PLANES]
+    lows = [net.send(own.at[p + (low, first)], ext.at[p + (low, outer)], net.leftward) for p in PLANES[LONG:]]
     for copy in inward:
         copy.wait()
     outward = [
@@ -410,39 +441,67 @@
     for copy in outward:
         copy.start()
     corners = []
-    for p, copy in zip(PLANES, tops):
-        copy.wait_recv()
+
+    def corner(n):
+        tops[n].wait_recv()
+        p = PLANES[n]
         corners.append(net.send(ext.at[p + (top, outer)], ext.at[p + (outer, outer)], net.over))
-    for copy in belows + lows + corners:
+
+    def reorder(f):
+        meas_out[f] = even_odd(meas[f], pick)
+
+    relay.forward()
+    corner(0)
+    turned = even_odd(phase[...], pick)
+    kern_out[0] = jnp.cos(turned)
+    kern_out[1] = jnp.sin(turned)
+    relay.forward()
+    corner(1)
+    reorder(0)
+    relay.forward()
+    corner(2)
+    reorder(1)
+    reorder(2)
+    relay.forward()
+    corner(3)
+    reorder(3)
+    for copy in belows + lows + corners + relay.hops:
         copy.wait_recv()
     for copy in outward:
         copy.wait()
     net.finish()
 
 
-def run_open(own):
+def run_open(own, phase, meas):
+    vmem = pl.BlockSpec(memory_space=pltpu.VMEM)
     anyw = pl.BlockSpec(memory_space=pl.ANY)
+    shape = jax.ShapeDtypeStruct
     return pl.pallas_call(
         open_kernel,
-        out_shape=jax.ShapeDtypeStruct((2, 2, 3 * K, 3 * K), F32),
-        in_specs=[anyw],
-        out_specs=anyw,
+        out_shape=[shape((2, 2, 3 * K, 3 * K), F32), shape((2, K, K), F32), shape(meas.shape, F32)],
+        in_specs=[anyw, vmem, vmem, vmem],
+        out_specs=[anyw, vmem, vmem],
         scratch_shapes=[
             pltpu.VMEM((2, 2, 2 * K, 2 * K), F32),
-            pltpu.SemaphoreType.DMA((16,)),
-            pltpu.SemaphoreType.DMA((16,)),
+            pltpu.VMEM((LONG, K, K), F32),
+            pltpu.VMEM((LONG, K, K), F32),
+            pltpu.SemaphoreType.DMA((24,)),
+            pltpu.SemaphoreType.DMA((24,)),
             pltpu.SemaphoreType.DMA((4,)),
         ],
         compiler_params=pltpu.CompilerParams(collective_id=2, has_side_effects=True, vmem_limit_bytes=48 << 20),
         name="open",
-    )(own)
+    )(own, phase, meas, even_odd_table())
 
 
 def exchange_kernel(final, *refs):
     es, beam, g, ext, beam_new, new = refs[:6]
     gov, grv, ov, rx, rbl, from_left, tr = refs[6:13]
     rest = refs[13:]
-    if not final:
+    if final:
+        way1, way2 = rest[:2]
+        rest = rest[2:]
+    else:
         rv, from_right, tl = rest[:3]
         rest = rest[3:]
     scale, rc, acc, rz, acc2, rxs, rys, total, ss, rs, ls = rest
@@ -539,6 +598,15 @@
             send(g.at[p + (outer, first)], rbl.at[p + (slice(None), first)], under),
         )
 
+    relays = []
+
+    def start_relay(_):
+        pieces = [(g.at[p + (low, outer)], from_left.at[p + (low,)]) for p in PLANES[:LONG]]
+        relays.append(Relay(net, way1, way2, leftward, pieces))
+
+    def forward(_):
+        relays[0].forward()
+
     def bottom(p):
         lows[p] = [send(g.at[p + (low, outer)], from_left.at[p + (low,)], rightward)]
         if not final:
@@ -585,7 +653,7 @@
             ups.append(send(ov.at[p + (top, mid)], new.at[p + (outer, mid)], over))
 
     def use_bottom(p):
-        for copy in lows[p]:
+        for copy in lows[p] if p in lows else [relays[0].hops[PLANES.index(p)]]:
             copy.wait_recv()
 
         def body(i):
@@ -627,13 +695,15 @@
 
     reduce_run = reduce_steps()
     acts = {"d": down, "b": bottom, "m": middle, "L": ready, "t": send_top, "M": use_middle, "B": use_bottom, "T": use_top, "U": settle}
-    done = {}
+    if final:
+        acts.update({"s": start_relay, "f": forward})
+    done = {"b": LONG - 1, "B": LONG - 1, "T": LONG - 1} if final else {}
     for turn in ORDER[final]:
         if turn == "r":
             next(reduce_run, None)
         else:
             done[turn] = done.get(turn, -1) + 1
-            acts[turn](PLANES[done[turn]])
+            acts[turn](PLANES[done[turn] % 4])
     for _ in reduce_run:
         pass
     net.finish()
@@ -646,7 +716,7 @@
     shape = jax.ShapeDtypeStruct
     square, strip = pltpu.VMEM((2, 2, tile, tile), F32), pltpu.VMEM((2, 2, tile, K), F32)
     flat, small = pltpu.VMEM((2, 2, K, tile), F32), pltpu.VMEM((2, 2, K, K), F32)
-    scratch = [square, strip, square, small, flat, strip, small] + ([] if final else [strip, strip, small])
+    scratch = [square, strip, square, small, flat, strip, small] + ([pltpu.VMEM((LONG, K, K), F32)] * 2 if final else [strip, strip, small])
     scratch += [
         pltpu.VMEM((8, K), F32),
         pltpu.VMEM((UNITS // 2, 8, HALF), F32),
@@ -677,13 +747,10 @@
 def shards(object_field, probe, kernel_phase, measured, positions, batch):
     tile = object_field.shape[2]
     tables = constants()
-    phase = even_odd(kernel_phase)
-    kern = jnp.stack([jnp.cos(phase), jnp.sin(phase)])
-    meas = even_odd(measured)
     corner = jnp.stack([lax.axis_index("tile") * tile, lax.axis_index("slab") * tile])
     local_at = positions - corner[None, :].astype(jnp.int32)
     beam = probe.reshape(2, K, 2, HALF).transpose(0, 2, 1, 3)
-    ext = run_open(object_field)
+    ext, kern, meas = run_open(object_field, kernel_phase, measured)
     for batch_no in range(BATCHES):
         grads, es = run_batch(batch_no, local_at, batch, ext, beam, kern, meas, tables)
         flat, ext = run_exchange(

time: 288 us -> 278 us (0.965)
  matrix products: 9.18 us -> 0 us
  local copies, waits for them, and re-layouts: 7.34 us -> 12.7 us
  Pallas kernels: 269 us -> 265 us
    dot_general x4 -> x0, matrix products: 9.18 us -> none  [the longest x2 4.65 us: even_odd(): jnp.einsum('kn,...kc->...nc', pick, value, precision=lax.Precision.HIGHEST)]
    unnamed x17 -> x23, local copies, waits for them, and re-layouts: 6.31 us -> 11.7 us
    pallas_call x1, Pallas kernels: 46.1 us -> 41.4 us  [run_open(): pl.pallas_call(open_kernel, out_shape=[shape((2, 2, 3 * K, 3 * K), F32),...]
where the time goes in v4:
time: 278 us
  Pallas kernels  265 us (95%)
  local copies, waits for them, and re-layouts  12.7 us (5%)
    pallas_call x2, Pallas kernels, run_exchange(): pl.pallas_call(functools.partial(exchange_kernel, final), out_shape=[shap...  186 us
    pallas_call x1, Pallas kernels, run_open(): pl.pallas_call(open_kernel, out_shape=[shape((2, 2, 3 * K, 3 * K), F32),...  41.4 us
    pallas_call x2, Pallas kernels, run_batch(): pl.pallas_call(functools.partial(batch_kernel, batch_no), out_shape=[jax....  37.3 us
    unnamed x23, local copies, waits for them, and re-layouts  11.7 us

profile of v4, /device:TPU:1, one launch (start us, length us, event | category | flops | bytes accessed | tf_op | source)
XLA Modules:
  0.0 278.3 jit_solution(18068651016386519451)
XLA Ops:
  0.6 0.1 pad_add_fusion
  0.7 0.8 copy.17
  1.5 1.2 copy.18
  2.7 0.2 copy.19
  2.9 0.0 copy-start
  2.9 1.2 copy-done
  4.2 0.0 copy-start.1
  4.2 0.9 copy-done.1
  5.1 0.0 copy-start.2
  5.1 0.9 copy-done.2
  6.1 41.4 %open.1 = (f32[2,2,768,768]{3,2,1,0:T(8,128)}, f32[2,256,256]{2,1,0:T(8,128)S(1)}, f32[4,256,256]{2,1,0:T(8,128)S(1)}) custom-call(f32[2,2,512,512]{3,2,1,0:T(8,128)} %own.1, f32[256,256]{1,0:T(8,128)S(1)} %copy-done.1, f32[4,256,256]{2,1,0:T(8,128)S(1)} %copy-done, bf16[2,256,256]{2,1,0:T(8,128)(2,1)S(1)} %copy-done.2), custom_call_target="tpu_custom_call" | custom-call | tf_op jit(solution)/shard_map/open/pallas_call | solution.py:479
  47.5 0.0 copy-start.3
  47.5 0.6 copy-done.3
  48.1 0.0 copy-start.4
  48.1 1.1 copy-done.4
  49.3 0.0 copy-start.6
  49.3 1.1 copy-done.6
  50.4 0.0 copy-start.8
  50.4 0.9 copy-done.8
  51.3 0.0 copy-start.9
  51.3 0.7 copy-done.9
  52.0 32.1 %frames.2 = (f32[2,2,768,768]{3,2,1,0:T(8,128)}, f32[3,2,256,128]{3,2,1,0:T(8,128)S(1)}) custom-call(s32[4,2]{1,0:T(4,128)S(1)} %broadcast_subtract_fusion.at_ref, s32[4]{0:T(128)S(1)} %copy-done.3, f32[2,2,768,768]{3,2,1,0:T(8,128)} %get-tuple-element.13.ext.refs_3_, f32[2,2,256,128]{3,2,1,0:T(8,128)S(1)} %bitcast.16, ...), custom_call_target="tpu_custom_call" | custom-call | flops 20000000000 | bytes 25165824 | tf_op jit(solution)/shard_map/frames/pallas_call | solution.py:343
  84.1 0.0 copy-start.5
  84.1 0.0 copy-start.7
  84.1 94.7 %exchange.1 = (f32[128,8,128]{2,1,0:T(8,128)S(1)}, f32[2,2,768,768]{3,2,1,0:T(8,128)}) custom-call(f32[192,8,128]{2,1,0:T(8,128)S(1)} %bitcast.19, f32[128,8,128]{2,1,0:T(8,128)S(1)} %bitcast.17, f32[2,2,768,768]{3,2,1,0:T(8,128)} %get-tuple-element.17.refs_2_, f32[2,2,768,768]{3,2,1,0:T(8,128)} %get-tuple-element.13.ext.refs_3_), custom_call_target="tpu_custom_call" | custom-call | tf_op jit(solution)/shard_map/exchange/pallas_call | solution.py:734
  178.8 0.0 copy-done.5
  178.8 0.0 copy-done.7
  178.9 5.2 %frames.3 = (f32[2,2,768,768]{3,2,1,0:T(8,128)}, f32[3,2,256,128]{3,2,1,0:T(8,128)S(1)}) custom-call(s32[4,2]{1,0:T(4,128)S(1)} %broadcast_subtract_fusion.at_ref, s32[4]{0:T(128)S(1)} %copy-done.3, f32[2,2,768,768]{3,2,1,0:T(8,128)} %get-tuple-element.18.ext.refs_3_, f32[2,2,256,128]{3,2,1,0:T(8,128)S(1)} %bitcast.20, ...), custom_call_target="tpu_custom_call" | custom-call | flops 20000000000 | bytes 25165824 | tf_op jit(solution)/shard_map/frames/pallas_call | solution.py:343
  184.1 91.3 %close.1 = (f32[128,8,128]{2,1,0:T(8,128)S(1)}, f32[2,2,512,512]{3,2,1,0:T(8,128)S(1)}) custom-call(f32[192,8,128]{2,1,0:T(8,128)S(1)} %bitcast.18, f32[128,8,128]{2,1,0:T(8,128)S(1)} %get-tuple-element.19.refs_1_, f32[2,2,768,768]{3,2,1,0:T(8,128)} %get-tuple-element.21.refs_2_, f32[2,2,768,768]{3,2,1,0:T(8,128)} %get-tuple-element.18.ext.refs_3_), custom_call_target="tpu_custom_call" | custom-call | tf_op jit(solution)/shard_map/close/pallas_call | solution.py:734
  275.4 0.8 copy.23
  276.3 2.0 copy.25
  (1 shorter events, 0.0 us)
Async XLA Ops:
  2.9 1.2 copy-start
  4.2 0.9 copy-start.1
  5.1 0.9 copy-start.2
  47.5 0.7 copy-start.3
  48.1 1.1 copy-start.4
  49.3 1.1 copy-start.6
  50.4 0.9 copy-start.8
  51.3 0.7 copy-start.9
  84.1 94.7 %copy-start.5 = (bf16[2,256,768]{2,1,0:T(8,128)(2,1)S(1)}, bf16[2,256,768]{2,1,0:T(8,128)(2,1)}, u32[]{:S(2)}) copy-start(bf16[2,256,768]{2,1,0:T(8,128)(2,1)} %constant.46.ml_ref) | copy-start | bytes 2359300
  84.1 94.7 %copy-start.7 = (bf16[2,768,256]{2,1,0:T(8,128)(2,1)S(1)}, bf16[2,768,256]{2,1,0:T(8,128)(2,1)}, u32[]{:S(2)}) copy-start(bf16[2,768,256]{2,1,0:T(8,128)(2,1)} %constant.41.mr_ref) | copy-start | bytes 2359300
